TPU v7x, 8 devices: a whole 2x2x1 slice. The times are simulated.
8 devices in a mesh: batch: 1 (over z), col: 2 (over y), row: 4 (over x, core).
Axes of the slice: x: 2, y: 2, z: 1, core: 2. Of those that a mesh axis runs over, the one named last changes fastest.
Arguments:
- lower_cyc: float32 [1536, 1536], P(('batch', 'row'), 'col')
Outputs:
- output: float32 [1536, 1536], P(('batch', 'row'), 'col')
All inputs are finite; a program needn't handle non-finite values.
Results may differ from a plain program's by a relative error of at most 0.001.
Values sent between devices are 32-bit elements.
A program may use at most 1 GiB of HBM per device.

v0:
```python
import jax
import jax.numpy as jnp
from jax import lax
from jax.sharding import PartitionSpec as P

DEPTH = 3
BLK = 8


def highest_matmul(left, right):
    return jnp.einsum("sik,skj->sij", left, right, precision=lax.Precision.HIGHEST, preferred_element_type=jnp.float32)


def natural_inner_cols(gathered):
    num_sub, row_len, grid_len, col_len = gathered.shape
    split_view = gathered.reshape(num_sub, row_len, grid_len, col_len // BLK, BLK)
    return split_view.transpose(0, 1, 3, 2, 4).reshape(num_sub, row_len, grid_len * col_len)


def natural_inner_rows(gathered):
    num_sub, grid_len, row_len, col_len = gathered.shape
    split_view = gathered.reshape(num_sub, grid_len, row_len // BLK, BLK, col_len)
    return split_view.transpose(0, 2, 1, 3, 4).reshape(num_sub, grid_len * row_len, col_len)


def cyclic_product(left, right):
    left_panel = natural_inner_cols(lax.all_gather(left, "col", axis=2))
    right_panel = natural_inner_rows(lax.all_gather(right, "row", axis=1))
    return highest_matmul(left_panel, right_panel)


def leaf_inverses(local_l, grid_rows, grid_cols):
    row_idx = lax.axis_index("row")
    col_idx = lax.axis_index("col")
    leaves = 2 ** DEPTH
    row_len = local_l.shape[0] // leaves
    col_len = local_l.shape[1] // leaves
    blocks4 = local_l.reshape(leaves, row_len, leaves, col_len)
    diag_blocks = jnp.stack([blocks4[leaf_idx, :, leaf_idx, :] for leaf_idx in range(leaves)])
    gathered = lax.all_gather(lax.all_gather(diag_blocks, "row", axis=1), "col", axis=3)
    leaf_size = grid_rows * row_len
    split_view = gathered.reshape(leaves, grid_rows, row_len // BLK, BLK, grid_cols, col_len // BLK, BLK)
    natural = split_view.transpose(0, 2, 1, 3, 5, 4, 6).reshape(leaves, leaf_size, leaf_size)
    piece_len = col_len // grid_rows
    local_cols = row_idx * piece_len + jnp.arange(piece_len)
    target_cols = (local_cols // BLK) * (grid_cols * BLK) + col_idx * BLK + local_cols % BLK
    identity_cols = (jnp.arange(leaf_size)[:, None] == target_cols[None, :]).astype(jnp.float32)
    rhs_batch = jnp.broadcast_to(identity_cols, (leaves, leaf_size, piece_len))
    solved = lax.linalg.triangular_solve(natural, rhs_batch, left_side=True, lower=True)
    parted = solved.reshape(leaves, row_len // BLK, grid_rows, BLK, piece_len)
    owned_rows = lax.all_to_all(parted, "row", 2, 4, tiled=True)
    return owned_rows.reshape(leaves, row_len, col_len)


def solution(mesh):
    grid_rows = mesh.shape["row"]
    grid_cols = mesh.shape["col"]
    block_spec = P(("batch", "row"), "col")

    def device_body(local_l):
        inverse = leaf_inverses(local_l, grid_rows, grid_cols)
        for level_idx in reversed(range(DEPTH)):
            num_sub = 2 ** level_idx
            half_rows = inverse.shape[1]
            half_cols = inverse.shape[2]
            paired_inv = inverse.reshape(num_sub, 2, half_rows, half_cols)
            inv_upper = paired_inv[:, 0]
            inv_lower = paired_inv[:, 1]
            blocks6 = local_l.reshape(num_sub, 2, half_rows, num_sub, 2, half_cols)
            coupling = jnp.stack([blocks6[sub_idx, 1, :, sub_idx, 0, :] for sub_idx in range(num_sub)])
            temp_prod = cyclic_product(coupling, inv_upper)
            off_diag = -cyclic_product(inv_lower, temp_prod)
            upper_rows = jnp.concatenate([inv_upper, jnp.zeros_like(inv_upper)], axis=2)
            lower_rows = jnp.concatenate([off_diag, inv_lower], axis=2)
            inverse = jnp.concatenate([upper_rows, lower_rows], axis=1)
        return inverse.reshape(local_l.shape)

    return jax.shard_map(device_body, mesh=mesh, in_specs=(block_spec,), out_specs=block_spec, check_vma=False)
```

profile of v0, /device:TPU:0, one launch (start us, length us, event | category | flops | bytes accessed | tf_op | source)
XLA Modules:
  0.0 427.8 jit_solution(6445657998294811923)
XLA Ops:
  6.5 1.9 reshape.155
  8.5 0.2 fusion.11
  8.8 13.0 %all-gather = f32[8,192,96]{2,1,0:T(8,128)S(1)} all-gather(f32[8,48,96]{2,1,0:T(8,128)S(1)} %constant_dynamic-update-slice_fusion), channel_id=2, replica_groups=mesh['batch'=1,'col'=2,'row'=4] {'row'}, dimensions={1}, use_global_device_ids=true | all-gather | bytes 737280 | tf_op jit(solution)/shard_map/all_gather | solution.py:40
  21.8 2.3 copy.213
  24.2 1.2 copy-done
  25.4 3.6 reshape.161
  28.9 1.4 reshape.171
  30.3 0.9 fusion.10
  31.3 0.1 copy.230
  31.5 0.1 slice_bitcast_fusion.12
  31.7 0.2 pad_maximum_fusion.2
  31.9 35.6 %all-gather.17.cloned.1.call-done = f32[8,4,48,192]{2,0,1,3:T(8,128)} async-done(((f32[8,4,48,96]{2,0,1,3:T(8,128)}), f32[8,4,48,192]{2,0,1,3:T(8,128)}) %all-gather.17.cloned.1.call-update) | async-done | bytes 1179664 | tf_op jit(solution)/shard_map/all_gather | solution.py:40
  67.5 2.9 copy.214
  70.3 16.1 %reshape.156 = f32[8,4,6,8,2,12,8]{6,5,4,3,2,1,0:T(8,128)} reshape(f32[8,4,48,192]{3,2,1,0:T(8,128)S(1)} %copy.214) | data formatting | bytes 2359296 | tf_op jit(solution)/shard_map/reshape | solution.py:42
  86.4 27.3 %copy.215 = f32[8,6,4,8,12,2,8]{6,5,4,3,2,1,0:T(2,128)} copy(f32[8,6,4,8,12,2,8]{6,4,5,3,1,2,0:T(8,128)} %bitcast.163) | data formatting | bytes 2359296 | tf_op jit(solution)/shard_map/transpose | solution.py:43
  113.7 25.2 %reshape.157 = f32[8,192,192]{2,1,0:T(8,128)S(1)} reshape(f32[8,6,4,8,12,2,8]{6,5,4,3,2,1,0:T(2,128)} %copy.215) | data formatting | bytes 2359296 | tf_op jit(solution)/shard_map/reshape | solution.py:43
  138.9 0.1 broadcast_select_fusion
  139.1 0.2 fusion.4
  139.4 0.9 copy-done.1
  140.3 157.9 %custom-call.3 = f32[8,2,128,128]{2,3,1,0:T(8,128)} custom-call(f32[8,2,128,128]{3,2,1,0:T(8,128)S(1)} %pad_maximum_fusion), custom_call_target="InvertDiagBlocksLowerTriangular" | custom-call | tf_op jit(solution)/shard_map/triangular_solve | solution.py:49
  298.2 1.6 fusion.3
  299.8 1.5 convolution_subtract_fusion
  301.3 1.3 fusion.6
  302.6 0.3 copy.219
  302.9 1.2 reshape.243
  304.2 3.3 all-to-all-start
  307.6 8.1 %all-gather.3 = f32[4,48,192]{1,0,2:T(4,128)S(1)} all-gather(f32[4,48,96]{1,0,2:T(4,128)S(1)} %copy.230), channel_id=5, replica_groups=mesh['batch'=1,'col'=2,'row'=4] {'col'}, dimensions={2}, use_global_device_ids=true | all-gather | bytes 221184 | tf_op jit(solution)/shard_map/all_gather | solution.py:27
  315.8 0.2 copy.243
  315.9 7.0 %all-gather.6 = f32[2,96,384]{1,0,2:T(2,128)S(1)} all-gather(f32[2,96,192]{1,0,2:T(2,128)S(1)} %copy.243), channel_id=8, replica_groups=mesh['batch'=1,'col'=2,'row'=4] {'col'}, dimensions={2}, use_global_device_ids=true | all-gather | bytes 442368 | tf_op jit(solution)/shard_map/all_gather | solution.py:27
  323.0 0.5 broadcast.157
  323.5 1.0 reduce
  324.6 0.6 reshape.244
  325.2 0.5 copy.221
  325.7 0.4 reshape_reshape.3
  326.1 9.3 %all_gather.70 = f32[4,4,48,96]{3,2,0,1:T(8,128)S(1)} all-gather(f32[4,1,48,96]{3,2,0,1:T(8,128)S(1)} %get-tuple-element.47), channel_id=1, replica_groups=mesh['batch'=1,'col'=2,'row'=4] {'row'}, dimensions={1}, use_global_device_ids=true | all-gather | bytes 368640 | tf_op jit(solution)/shard_map/all_gather | solution.py:28
  335.5 0.8 fusion.12
  336.3 8.7 %all-gather.4 = f32[4,192,96]{2,1,0:T(8,128)S(1)} all-gather(f32[4,48,96]{2,1,0:T(8,128)S(1)} %fusion.12), channel_id=6, replica_groups=mesh['batch'=1,'col'=2,'row'=4] {'row'}, dimensions={1}, use_global_device_ids=true | all-gather | bytes 368640 | tf_op jit(solution)/shard_map/all_gather | solution.py:28
  345.0 0.1 copy.224
  345.2 6.3 %all-gather.2 = f32[4,1,48,192]{2,0,1,3:T(4,128)S(1)} all-gather(f32[4,1,48,96]{2,0,1,3:T(4,128)S(1)} %copy.224), channel_id=4, replica_groups=mesh['batch'=1,'col'=2,'row'=4] {'col'}, dimensions={3}, use_global_device_ids=true | all-gather | bytes 221184 | tf_op jit(solution)/shard_map/all_gather | solution.py:27
  351.6 0.8 convolution_negate_fusion.2
  352.4 0.1 select_maximum_fusion.3
  352.6 10.9 %all_gather.76 = f32[2,4,96,192]{3,2,0,1:T(8,128)S(1)} all-gather(f32[2,1,96,192]{3,2,0,1:T(8,128)S(1)} %get-tuple-element.43), channel_id=1, replica_groups=mesh['batch'=1,'col'=2,'row'=4] {'row'}, dimensions={1}, use_global_device_ids=true | all-gather | bytes 737280 | tf_op jit(solution)/shard_map/all_gather | solution.py:28
  363.6 0.8 fusion.13
  364.5 11.1 %all-gather.7 = f32[2,384,192]{2,1,0:T(8,128)S(1)} all-gather(f32[2,96,192]{2,1,0:T(8,128)S(1)} %fusion.13), channel_id=9, replica_groups=mesh['batch'=1,'col'=2,'row'=4] {'row'}, dimensions={1}, use_global_device_ids=true | all-gather | bytes 737280 | tf_op jit(solution)/shard_map/all_gather | solution.py:28
  375.6 0.2 copy.239
  375.8 6.3 %all-gather.5 = f32[2,1,96,384]{2,0,1,3:T(2,128)S(1)} all-gather(f32[2,1,96,192]{2,0,1,3:T(2,128)S(1)} %copy.239), channel_id=7, replica_groups=mesh['batch'=1,'col'=2,'row'=4] {'col'}, dimensions={3}, use_global_device_ids=true | all-gather | bytes 442368 | tf_op jit(solution)/shard_map/all_gather | solution.py:27
  382.2 0.9 convolution_negate_fusion.1
  383.1 0.1 fusion.2
  383.2 0.8 slice_bitcast_fusion.3
  384.0 0.6 reshape.183
  384.7 0.2 slice.138
  384.9 7.4 %all-gather.9 = f32[1,1,192,2,1,384]{5,2,4,1,0,3:T(8,128)S(1)} all-gather(f32[1,1,192,1,1,384]{5,2,4,1,0,3:T(8,128)S(1)} %copy.256), channel_id=11, replica_groups=mesh['batch'=1,'col'=2,'row'=4] {'col'}, dimensions={3}, use_global_device_ids=true | all-gather | bytes 884736 | tf_op jit(solution)/shard_map/all_gather | solution.py:27
  392.3 0.3 copy.257
  392.6 0.1 copy.258
  392.7 6.1 %all-gather.15.cloned.1.call-done = f32[1,4,192,384]{3,2,0,1:T(8,128)} async-done(((f32[1,1,192,384]{3,2,0,1:T(8,128)}), f32[1,4,192,384]{3,2,0,1:T(8,128)}) %all-gather.15.cloned.1.call-update) | async-done | bytes 1179664 | tf_op jit(solution)/shard_map/all_gather | solution.py:28
  398.8 1.4 copy.255
  400.2 2.3 convolution_bitcast_fusion
  402.6 9.8 %all-gather.8 = f32[1,1,192,768]{3,2,1,0:T(8,128)S(1)} all-gather(f32[1,1,192,384]{3,2,1,0:T(8,128)S(1)} %get-tuple-element.41), channel_id=10, replica_groups=mesh['batch'=1,'col'=2,'row'=4] {'col'}, dimensions={3}, use_global_device_ids=true | all-gather | bytes 884736 | tf_op jit(solution)/shard_map/all_gather | solution.py:27
  412.4 0.3 copy.252
  412.7 0.1 copy.253
  412.8 4.4 %all-gather.19.cloned.1.call-done = f32[768,384]{1,0:T(8,128)} async-done(((f32[192,384]{1,0:T(8,128)}), f32[768,384]{1,0:T(8,128)}) %all-gather.19.cloned.1.call-update) | async-done | bytes 1179664 | tf_op jit(solution)/shard_map/all_gather | solution.py:28
  417.2 1.4 copy.259
  418.6 1.6 fusion.1
  420.2 1.1 fusion
  (50 shorter events, 1.2 us)
Async XLA Ops:
  6.5 60.9 %all-gather.17.cloned.1.call-start = ((), (), s32[]{:S(2)}) async-start(), calls=%async_computation.2 | async-start | bytes 4718592 | tf_op jit(solution)/shard_map/all_gather | solution.py:40
  24.1 1.3 copy-start
  24.2 4.7 %copy-start.2 = (f32[192,24]{0,1:T(8,128)}, f32[192,24]{0,1:T(8,128)S(1)}, u32[]{:S(2)}) copy-start(f32[192,24]{0,1:T(8,128)S(1)} %fusion.8) | copy-start | bytes 55300
  139.1 1.2 copy-start.1
  140.2 157.9 %slice-start = ((f32[192,24]{0,1:T(8,128)}), f32[128,24]{0,1:T(8,128)S(1)}, s32[]{:S(2)}) async-start(f32[192,24]{0,1:T(8,128)} %copy-done.2), calls=%async_computation.4 | async-start | bytes 24576 | tf_op jit(solution)/shard_map/triangular_solve | solution.py:49
  140.2 159.5 %slice-start.1 = ((f32[192,24]{0,1:T(8,128)}), f32[64,24]{0,1:T(8,128)S(1)}, s32[]{:S(2)}) async-start(f32[192,24]{0,1:T(8,128)} %copy-done.2), calls=%async_computation.5 | async-start | bytes 24576 | tf_op jit(solution)/shard_map/triangular_solve | solution.py:49
  304.2 18.8 %all-to-all-start = ((f32[4,1,9216]{2,1,0:T(1,128)}), f32[4,1,9216]{2,1,0:T(1,128)S(1)}, u32[]{:S(2)}, u32[]{:S(2)}) async-start(f32[4,1,9216]{2,1,0:T(1,128)} %reshape.243), calls=%async_computation | async-start | bytes 294912 | tf_op jit(solution)/shard_map/all_to_all | solution.py:51
  307.5 91.3 %all-gather.15.cloned.1.call-start = ((), (), s32[]{:S(2)}) async-start(), calls=%async_computation.1 | async-start | bytes 1474560 | tf_op jit(solution)/shard_map/all_gather | solution.py:28
  384.0 33.2 %all-gather.19.cloned.1.call-start = ((), (), s32[]{:S(2)}) async-start(), calls=%async_computation.3 | async-start | bytes 1474560 | tf_op jit(solution)/shard_map/all_gather | solution.py:28
Sparse Core Ops, SparseCore 0:
  24.2 43.1 all-gather.16
  384.1 14.6 all-gather.14
  402.7 14.4 all-gather.18
where the time goes:
time: 428 us
  other arithmetic  161 us (38%)
  blocking collectives  98.1 us (23%)
  local copies, waits for them, and re-layouts  93.9 us (22%)
  waiting for transfers between devices  46.2 us (11%)
  between operations  13.6 us (3%)
  matrix products  11.7 us (3%)
    another operation x8, other arithmetic, leaf_inverses(): lax.linalg.triangular_solve(natural, rhs_batch, left_side=True, lower=True)  158 us
    all_gather x6, blocking collectives, cyclic_product(): left_panel = natural_inner_cols(lax.all_gather(left, 'col', axis=2))  45 us
    all_gather x4, blocking collectives, cyclic_product(): right_panel = natural_inner_rows(lax.all_gather(right, 'row', axis=1))  40 us
    all_gather x1, waiting for transfers between devices, leaf_inverses(): lax.all_gather(lax.all_gather(diag_blocks, 'row', axis=1), 'col', axis=3)  35.6 us
    transpose x1, local copies, waits for them, and re-layouts, leaf_inverses(): split_view.transpose(0, 2, 1, 3, 5, 4, 6)  27.3 us
    reshape x1, local copies, waits for them, and re-layouts, leaf_inverses(): split_view.transpose(0, 2, 1, 3, 5, 4, 6)  25.2 us
    reshape x1, local copies, waits for them, and re-layouts, leaf_inverses(): gathered.reshape(leaves, grid_rows, row_len // BLK, BLK, grid_cols, col_l...  16.1 us
    all_gather x1, blocking collectives, leaf_inverses(): lax.all_gather(diag_blocks, 'row', axis=1)  13 us
  transfers between devices with their start and end apart: 4, of which 3 were waited for; matrix products, arithmetic and copies ran while one was open for 2% of the time, Pallas kernels for 0%

commit v1 on v0

v1 whole, which is shorter than its diff:
```python
import jax
import jax.numpy as jnp
from jax import lax
from jax.experimental import pallas as pl
from jax.experimental.pallas import tpu as pltpu
from jax.sharding import PartitionSpec as P

MESH = pl.DeviceIdType.MESH
F32 = jnp.float32
AD, AO, BD, BO = range(4)
BLOCKS = (
    ((0, 0), (1, 1), (2, 2)),
    ((1, 0), (2, 0), (2, 1)),
    ((3, 3), (4, 4), (5, 5)),
    ((4, 3), (5, 3), (5, 4)),
)


def hdot(left, right):
    return jnp.dot(left, right, precision=lax.Precision.HIGHEST, preferred_element_type=F32)


def kernel(inp, out, gat, inv, cc, xa, tt, loc_sem, g_send, g_recv, c_send, c_recv, t_send, t_recv):
    row = lax.axis_index("row")
    y = lax.axis_index("col")
    x = row // 2
    c = row % 2
    xo, yo, co = 1 - x, 1 - y, 1 - c
    sib = {"row": 2 * x + co}
    xnb = {"row": 2 * xo + c}
    ynb = {"col": yo}

    def slot(g, sx, sc, sy, lo=0, num=8):
        return gat.at[g, sy, :, sc, pl.ds(lo, num), sx]

    local = {}
    for g in (AD, AO):
        local[g] = []
        for i, (bi, bj) in enumerate(BLOCKS[g]):
            local[g].append(pltpu.make_async_copy(
                inp.at[pl.ds(8 * bi, 8), :, pl.ds(128 * bj, 128)], gat.at[g, y, i, c, :, x], loc_sem.at[g, i]))
    local_c = [pltpu.make_async_copy(
        inp.at[pl.ds(24 + 8 * t, 8), :, pl.ds(0, 384)], cc.at[y, t], loc_sem.at[4, t]) for t in range(3)]
    for g in (BD, BO):
        local[g] = []
        for i, (bi, bj) in enumerate(BLOCKS[g]):
            local[g].append(pltpu.make_async_copy(
                inp.at[pl.ds(8 * bi, 8), :, pl.ds(128 * bj, 128)], gat.at[g, y, i, c, :, x], loc_sem.at[g, i]))
    for g in (AD, AO):
        for cp in local[g]:
            cp.start()
    for cp in local_c:
        cp.start()
    for g in (BD, BO):
        for cp in local[g]:
            cp.start()

    barrier = pltpu.get_barrier_semaphore()
    for nbr in (sib, xnb, ynb):
        pl.semaphore_signal(barrier, inc=1, device_id=nbr, device_id_type=MESH)
    pl.semaphore_wait(barrier, 3)

    sends = []

    def gsend(g, k, ref, dev):
        cp = pltpu.make_async_remote_copy(ref, ref, g_send.at[g, k], g_recv.at[g, k], device_id=dev, device_id_type=MESH)
        cp.start()
        sends.append(cp)

    def gwait(g, k, ref):
        pltpu.make_async_remote_copy(ref, ref, g_send.at[g, k], g_recv.at[g, k], device_id=sib,
                                     device_id_type=MESH).wait_recv()

    def own_x(g):
        gsend(g, 0, slot(g, x, c, y), xnb)

    def own_y(g):
        gsend(g, 1, slot(g, x, c, y), ynb)

    def own_s(g):
        gsend(g, 2, slot(g, x, c, y), sib)

    def wait_local(g):
        for cp in local[g]:
            cp.wait()

    def fwd_x(g):
        gwait(g, 0, slot(g, xo, c, y))
        gsend(g, 3, slot(g, xo, c, y, 0, 4), ynb)
        gsend(g, 5, slot(g, xo, c, y), sib)

    def fwd_y(g):
        gwait(g, 1, slot(g, x, c, yo))
        gsend(g, 4, slot(g, x, c, yo, 4, 4), xnb)
        gsend(g, 6, slot(g, x, c, yo), sib)

    def fwd_d(g):
        gwait(g, 3, slot(g, xo, c, yo, 0, 4))
        gsend(g, 7, slot(g, xo, c, yo, 0, 4), sib)
        gwait(g, 4, slot(g, xo, c, yo, 4, 4))
        gsend(g, 8, slot(g, xo, c, yo, 4, 4), sib)

    def wait_sib(g):
        gwait(g, 2, slot(g, x, co, y))
        gwait(g, 5, slot(g, xo, co, y))
        gwait(g, 6, slot(g, x, co, yo))
        gwait(g, 7, slot(g, xo, co, yo, 0, 4))
        gwait(g, 8, slot(g, xo, co, yo, 4, 4))

    def c_copy(t, q):
        return pltpu.make_async_remote_copy(cc.at[q, t], cc.at[q, t], c_send.at[t], c_recv.at[t], device_id=ynb,
                                            device_id_type=MESH)

    def send_c(t):
        local_c[t].wait()
        cp = c_copy(t, y)
        cp.start()
        sends.append(cp)

    sub = lax.broadcasted_iota(jnp.int32, (8, 128), 0)
    lane = lax.broadcasted_iota(jnp.int32, (8, 128), 1)
    seg = lane // 16

    def base(g, i, dst):
        low = [[None, None] for _ in range(4)]
        for nb in range(4):
            xr, qr = nb // 2, nb % 2
            for qc in range(2):
                acc = gat[g, qc, i, qr, 0, xr]
                for lb in range(1, 8):
                    acc = jnp.where(seg == lb, gat[g, qc, i, qr, lb, xr], acc)
                low[nb][qc] = acc
        rec = []
        for qc in range(2):
            dsum = jnp.zeros((8, 128), F32)
            for xr in range(2):
                here = (sub == lane % 8) & ((lane // 8) % 2 == xr)
                dsum = dsum + jnp.where(here, low[2 * xr + qc][qc], 0.0)
            rec.append(1.0 / jnp.sum(dsum, axis=0, keepdims=True))
        rhs = []
        for nb in range(4):
            for qc in range(2):
                low[nb][qc] = low[nb][qc] * rec[qc]
            rhs.append([jnp.where((sub == lane % 8) & ((lane // 8) % 2 == nb // 2), 1.0, 0.0) if nb % 2 == qc
                        else jnp.zeros((8, 128), F32) for qc in range(2)])
        for k in range(32):
            nk, ek = k // 8, k % 8
            xk, qk = nk // 2, nk % 2
            idx = 16 * seg + (8 * xk + ek)
            for nb in range(nk, 4):
                if nb == nk and ek == 7:
                    continue
                col = jnp.take_along_axis(low[nb][qk], idx, axis=1, mode="promise_in_bounds")
                if nb == nk:
                    col = jnp.where(sub > ek, col, 0.0)
                for qc in range(2):
                    rhs[nb][qc] = rhs[nb][qc] - col * rhs[nk][qc][ek:ek + 1, :]
        for nb in range(4):
            xr, qr = nb // 2, nb % 2
            idx = 16 * seg + 8 * xr + sub
            scale = jnp.take_along_axis(jnp.broadcast_to(rec[qr], (8, 128)), idx, axis=1, mode="promise_in_bounds")
            for qc in range(2):
                val = rhs[nb][qc] * scale
                for lb in range(8):
                    inv[dst, qc, qr, lb, xr] = jnp.where(seg == lb, val, 0.0)

    def both(ref_of):
        return jnp.concatenate([ref_of(0), ref_of(1)], axis=1)

    def inv_full(t):
        return both(lambda qc: inv[t, qc].reshape(256, 128))

    def gat_full(g, i):
        return both(lambda qc: gat[g, qc, i].reshape(256, 128))

    def double(g, w):
        first = 3 * (g // 2)
        odd = [(q, lb0) for q in range(2) for lb0 in range(w, 8, 2 * w)]
        temps = []
        for i in range(3):
            parts = []
            for q, lb0 in odd:
                rows = both(lambda qc: gat[g, qc, i, q, lb0:lb0 + w].reshape(16 * w, 128))
                col = lax.broadcasted_iota(jnp.int32, rows.shape, 1) % 128
                parts.append(jnp.where(col // (16 * w) == lb0 // w - 1, rows, 0.0))
            temps.append(hdot(jnp.concatenate(parts, axis=0), inv_full(first + i)))
        for i in range(3):
            parts = []
            full = []
            at = 0
            for q in range(2):
                for lb0 in range(0, 8, w):
                    if (lb0 // w) % 2 == 1:
                        full.append(temps[i][at:at + 16 * w])
                        at += 16 * w
                    else:
                        full.append(jnp.zeros((16 * w, 256), F32))
            for q, lb0 in odd:
                parts.append(both(lambda qc: inv[first + i, qc, q, lb0:lb0 + w].reshape(16 * w, 128)))
            left = jnp.concatenate(parts, axis=0)
            new = left - hdot(left, jnp.concatenate(full, axis=0))
            at = 0
            for q, lb0 in odd:
                piece = new[at:at + 16 * w]
                at += 16 * w
                for qc in range(2):
                    inv[first + i, qc, q, lb0:lb0 + w] = piece[:, 128 * qc:128 * qc + 128].reshape(w, 2, 8, 128)

    def diag_inverses(g):
        for i in range(3):
            base(g, i, 3 * (g // 2) + i)
        for w in (1, 2, 4):
            double(g, w)

    wait_local(AD)
    own_x(AD)
    own_y(AD)
    own_s(AD)
    wait_local(AO)
    own_x(AO)
    own_y(AO)
    own_s(AO)
    fwd_x(AD)
    fwd_y(AD)
    wait_local(BD)
    own_x(BD)
    send_c(0)
    fwd_x(AO)
    fwd_y(AO)
    wait_local(BO)
    own_x(BO)
    send_c(1)
    send_c(2)
    own_y(BD)
    own_y(BO)
    own_s(BD)
    own_s(BO)
    fwd_d(AD)
    wait_sib(AD)
    diag_inverses(AD)
    fwd_d(AO)
    wait_sib(AO)

    def inv_y(t):
        return inv[t, y].reshape(256, 128)

    x00, x11, x22 = inv_y(0), inv_y(1), inv_y(2)
    xa[0, :, 0:128] = x00
    xa[1, :, 128:256] = x11
    xa[2, :, 256:384] = x22
    x10 = -hdot(inv_full(1), hdot(gat_full(AO, 0), x00))
    xa[1, :, 0:128] = x10
    x1 = jnp.concatenate([x10, x11], axis=1)
    t20 = hdot(gat_full(AO, 2), x1)
    t20 = t20 + jnp.concatenate([hdot(gat_full(AO, 1), x00), jnp.zeros((256, 128), F32)], axis=1)
    xa[2, :, 0:256] = -hdot(inv_full(2), t20)

    def t_ref(t, sx, sc):
        return tt.at[t, sc, :, sx]

    def t_copy(k, t, sx, sc, dev):
        ref = t_ref(t, sx, sc)
        return pltpu.make_async_remote_copy(ref, ref, t_send.at[k, t], t_recv.at[k, t], device_id=dev,
                                            device_id_type=MESH)

    def t_start(k, t, sx, sc, dev):
        cp = t_copy(k, t, sx, sc, dev)
        cp.start()
        sends.append(cp)

    for t in range(3):
        c_copy(t, yo).wait_recv()
        acc = [None] * 3
        for u in range(3):
            left = both(lambda q: cc[q, t, :, :, 128 * u:128 * u + 128].reshape(64, 128))
            prod = hdot(left, xa[u, :, 0:128 * (u + 1)])
            for j in range(u + 1):
                part = prod[:, 128 * j:128 * j + 128]
                acc[j] = part if acc[j] is None else acc[j] + part
        tt[t, c, :, x] = jnp.concatenate(acc, axis=1).reshape(8, 8, 384)
        t_start(0, t, x, c, xnb)
        t_start(1, t, x, c, sib)

    fwd_x(BD)
    fwd_x(BO)
    fwd_y(BD)
    fwd_y(BO)
    fwd_d(BD)
    wait_sib(BD)
    diag_inverses(BD)
    fwd_d(BO)
    for t in range(3):
        t_copy(0, t, xo, c, sib).wait_recv()
        t_start(2, t, xo, c, sib)
    wait_sib(BO)

    def z_diag(t):
        return both(lambda qc: inv[t, qc, c, :, x].reshape(64, 128))

    z22, z33 = z_diag(4), z_diag(5)
    w10 = hdot(gat_full(BO, 0), inv_full(3))
    w20 = hdot(gat_full(BO, 1), inv_full(3))
    w21 = hdot(gat_full(BO, 2), inv_full(4))
    z10 = -hdot(z22, w10)
    v10 = -hdot(inv_full(4), w10)
    z21 = -hdot(z33, w21)
    z20 = -hdot(z33, w20 + hdot(gat_full(BO, 2), v10))
    zrow = ((z_diag(3),), (z10, z22), (z20, z21, z33))

    zero = jnp.zeros((64, 128), F32)
    xa_rows = xa.reshape(3, 2, 8, 2, 8, 384)
    for t in range(3):
        rows_a = xa_rows[t, c, :, x].reshape(64, 384)
        for j in range(3):
            out[64 * t:64 * t + 64, 128 * j:128 * j + 128] = rows_a[:, 128 * j:128 * j + 128] if j <= t else zero
            if j <= t:
                blk = zrow[t][j]
                blk = jnp.where(y == 0, blk[:, 0:128], blk[:, 128:256])
            else:
                blk = zero
            out[192 + 64 * t:256 + 64 * t, 384 + 128 * j:512 + 128 * j] = blk
        out[64 * t:64 * t + 64, 384:768] = jnp.zeros((64, 384), F32)

    acc = [None] * 3
    for t in range(3):
        t_copy(1, t, x, co, sib).wait_recv()
        t_copy(2, t, xo, co, sib).wait_recv()
        left = jnp.concatenate([zrow[s][t] for s in range(t, 3)], axis=0)
        prod = hdot(left, tt[t].reshape(256, 384))
        for s in range(t, 3):
            part = prod[64 * (s - t):64 * (s - t) + 64]
            acc[s] = part if acc[s] is None else acc[s] + part
        out[192 + 64 * t:256 + 64 * t, 0:384] = -acc[t]

    for cp in sends:
        cp.wait_send()


def solution(mesh):
    spec = P(("batch", "row"), "col")

    def body(local_l):
        rows, cols = local_l.shape
        return pl.pallas_call(
            kernel,
            out_shape=jax.ShapeDtypeStruct((rows, cols), F32),
            in_specs=[pl.BlockSpec(memory_space=pl.ANY)],
            out_specs=pl.BlockSpec(memory_space=pltpu.VMEM),
            scratch_shapes=[
                pltpu.VMEM((4, 2, 3, 2, 8, 2, 8, 128), F32),
                pltpu.VMEM((6, 2, 2, 8, 2, 8, 128), F32),
                pltpu.VMEM((2, 3, 8, 8, 384), F32),
                pltpu.VMEM((3, 256, 384), F32),
                pltpu.VMEM((3, 2, 8, 2, 8, 384), F32),
                pltpu.SemaphoreType.DMA((5, 3)),
                pltpu.SemaphoreType.DMA((4, 9)),
                pltpu.SemaphoreType.DMA((4, 9)),
                pltpu.SemaphoreType.DMA((3,)),
                pltpu.SemaphoreType.DMA((3,)),
                pltpu.SemaphoreType.DMA((3, 3)),
                pltpu.SemaphoreType.DMA((3, 3)),
            ],
            compiler_params=pltpu.CompilerParams(
                collective_id=0, has_side_effects=True, vmem_limit_bytes=40 * 1024 * 1024),
        )(local_l.reshape(rows // 8, 8, cols))

    return jax.shard_map(body, mesh=mesh, in_specs=(spec,), out_specs=spec, check_vma=False)
```

time: 428 us -> 41.6 us (0.10)
  other arithmetic: 161 us -> 0 us
  blocking collectives: 98.1 us -> 0 us
  local copies, waits for them, and re-layouts: 93.9 us -> 2.29 us
  waiting for transfers between devices: 46.2 us -> 0 us
  Pallas kernels: 0 us -> 39.2 us
  between operations: 13.6 us -> 0.01 us
  matrix products: 11.7 us -> 0 us
    another operation x10 -> x0, other arithmetic: 159 us -> none  [the longest x8 158 us: leaf_inverses(): lax.linalg.triangular_solve(natural, rhs_batch, left_side=True, lower=True)]
    all_gather x11 -> x0, blocking collectives: 98.1 us -> none  [the longest x6 45 us: cyclic_product(): left_panel = natural_inner_cols(lax.all_gather(left, 'col', axis=2))]
    reshape x11 -> x0, local copies, waits for them, and re-layouts: 50.5 us -> none  [the longest x1 25.2 us: leaf_inverses(): split_view.transpose(0, 2, 1, 3, 5, 4, 6)]
    all_gather x3 -> x0, waiting for transfers between devices: 46.2 us -> none  [the longest x1 35.6 us: leaf_inverses(): lax.all_gather(lax.all_gather(diag_blocks, 'row', axis=1), 'col', axis=3)]
    pallas_call x0 -> x1, Pallas kernels: none -> 39.2 us  [body(): pl.pallas_call(kernel, out_shape=jax.ShapeDtypeStruct((rows, cols), F32),...]
    transpose x9 -> x0, local copies, waits for them, and re-layouts: 29.1 us -> none  [the longest x1 27.3 us: leaf_inverses(): split_view.transpose(0, 2, 1, 3, 5, 4, 6)]
    dot_general x6 -> x0, matrix products: 7.27 us -> none  [highest_matmul(): jnp.einsum('sik,skj->sij', left, right, precision=lax.Precision.HIGHEST,...]
    all_gather x8 -> x0, local copies, waits for them, and re-layouts: 5.81 us -> none  [the longest x1 2.87 us: leaf_inverses(): lax.all_gather(lax.all_gather(diag_blocks, 'row', axis=1), 'col', axis=3)]
  transfers between devices with their start and end apart: 4 -> 0, of which waited for: 3 -> 0; matrix products, arithmetic and copies ran while one was open for 2% -> 0% of each run, Pallas kernels for 0% -> 0%
where the time goes in v1:
time: 41.6 us; the launch traced here: 41.5 us
  Pallas kernels  39.2 us (94%)
  local copies, waits for them, and re-layouts  2.29 us (6%)
    pallas_call x1, Pallas kernels, body(): pl.pallas_call(kernel, out_shape=jax.ShapeDtypeStruct((rows, cols), F32),...  39.2 us
    unnamed x3, local copies, waits for them, and re-layouts  2.29 us

profile of v1, /device:TPU:0, one launch (start us, length us, event | category | flops | bytes accessed | tf_op | source)
XLA Modules:
  0.0 41.5 jit_solution(5572141760258592489)
XLA Ops:
  0.0 0.0 copy-start
  0.0 1.3 %copy-done = f32[384,768]{1,0:T(8,128)S(1)} copy-done((f32[384,768]{1,0:T(8,128)S(1)}, f32[384,768]{1,0:T(8,128)}, u32[]{:S(2)}) %copy-start) | copy-done | bytes 1179672
  1.3 39.2 %shard_map.17 = f32[384,768]{1,0:T(8,128)S(1)} custom-call(f32[48,8,768]{2,1,0:T(8,128)S(1)} %bitcast.1), custom_call_target="tpu_custom_call" | custom-call | tf_op jit(solution)/shard_map/pallas_call | solution.py:344
  40.5 1.0 %copy.3 = f32[384,768]{1,0:T(8,128)} copy(f32[384,768]{1,0:T(8,128)S(1)} %shard_map.17) | data formatting | bytes 2359296
Async XLA Ops:
  0.0 1.3 %copy-start = (f32[384,768]{1,0:T(8,128)S(1)}, f32[384,768]{1,0:T(8,128)}, u32[]{:S(2)}) copy-start(f32[384,768]{1,0:T(8,128)} %param.1) | copy-start | bytes 3538948

commit v2 on v0

v2 whole, which is shorter than its diff:
```python
import jax
import jax.numpy as jnp
from jax import lax
from jax.experimental import pallas as pl
from jax.experimental.pallas import tpu as pltpu
from jax.sharding import PartitionSpec as P

MESH = pl.DeviceIdType.MESH
F32 = jnp.float32
DIAG = ((5, 4, 3), (2, 1, 0))
OFF = (
    ((5, 4), (5, 3), (4, 3)),
    ((5, 2), (4, 2), (3, 2)),
    ((5, 1), (4, 1), (3, 1)),
    ((2, 1), (5, 0), (4, 0)),
    ((3, 0), (2, 0), (1, 0)),
)
D1, D2, O1, O2, O3, O4, O5 = range(7)
OFF_AT = {blk: 3 * g + i for g, grp in enumerate(OFF) for i, blk in enumerate(grp)}
DIAG_AT = {blk: (g, i) for g, grp in enumerate(DIAG) for i, blk in enumerate(grp)}


def hdot(left, right):
    return jnp.dot(left, right, precision=lax.Precision.HIGHEST, preferred_element_type=F32)


def kernel(inp, out, raw, dpk, dg, goff, inv, loc_sem, g_send, g_recv):
    row = lax.axis_index("row")
    y = lax.axis_index("col")
    x = row // 2
    c = row % 2
    xo, yo, co = 1 - x, 1 - y, 1 - c
    sib = {"row": 2 * x + co}
    xnb = {"row": 2 * xo + c}
    ynb = {"col": yo}

    def take(bi, bj, dst, sem):
        return pltpu.make_async_copy(inp.at[pl.ds(8 * bi, 8), :, pl.ds(128 * bj, 128)], dst, sem)

    local = {}
    for g, grp in enumerate(DIAG):
        local[g] = [take(b, b, raw.at[b], loc_sem.at[b]) for b in grp]
    for g, grp in enumerate(OFF):
        local[2 + g] = [take(bi, bj, goff.at[3 * g + i, y, c, :, x], loc_sem.at[6 + 3 * g + i])
                        for i, (bi, bj) in enumerate(grp)]
    for g in range(7):
        for cp in local[g]:
            cp.start()

    barrier = pltpu.get_barrier_semaphore()
    for nbr in (sib, xnb, ynb):
        pl.semaphore_signal(barrier, inc=1, device_id=nbr, device_id_type=MESH)

    sub = lax.broadcasted_iota(jnp.int32, (8, 128), 0)
    lane = lax.broadcasted_iota(jnp.int32, (8, 128), 1)

    def lanes(shape):
        return lax.broadcasted_iota(jnp.int32, shape, len(shape) - 1)

    def along(tile, idx):
        return jnp.take_along_axis(tile, idx, axis=1, mode="promise_in_bounds")

    def turn(tile, n):
        return along(tile, (lanes(tile.shape) + (128 - n)) & 127)

    def pack(g):
        for cp in local[g]:
            cp.wait()
        for i, b in enumerate(DIAG[g]):
            dpk[g, y, c, x, 5 * i] = raw[b, 7]
            for p in range(3):
                n = 112 - 16 * p
                dpk[g, y, c, x, 5 * i + 1 + p] = jnp.where(lane < n, raw[b, 6 - p], turn(raw[b, p], n))
            dpk[g, y, c, x, 5 * i + 4] = raw[b, 3]

    def unpack(g):
        for i in range(3):
            for qc in range(2):
                for lb in range(8):
                    if lb >= 3:
                        tiles = dpk[g, qc, :, :, 5 * i + 7 - lb]
                    else:
                        tiles = dpk[g, qc, :, :, 5 * i + 1 + lb].reshape(32, 128)
                        tiles = turn(tiles, 16 * (lb + 1)).reshape(2, 2, 8, 128)
                    dg[g, i, qc, :, lb] = tiles

    def slot(g, sx, sc, sy, half=None):
        if g < 2:
            lo, num = (0, 15) if half is None else ((0, 8), (8, 7))[half]
            return dpk.at[g, sy, sc, sx, pl.ds(lo, num)]
        lo, num = (0, 8) if half is None else (4 * half, 4)
        return goff.at[pl.ds(3 * (g - 2), 3), sy, sc, pl.ds(lo, num), sx]

    sends = []

    def gsend(g, k, ref, dev):
        cp = pltpu.make_async_remote_copy(ref, ref, g_send.at[g, k], g_recv.at[g, k], device_id=dev, device_id_type=MESH)
        cp.start()
        sends.append(cp)

    def gwait(g, k, ref):
        pltpu.make_async_remote_copy(ref, ref, g_send.at[g, k], g_recv.at[g, k], device_id=sib,
                                     device_id_type=MESH).wait_recv()

    def own(g):
        if g >= 2:
            for cp in local[g]:
                cp.wait()
        gsend(g, 0, slot(g, x, c, y), xnb)
        gsend(g, 1, slot(g, x, c, y), ynb)
        gsend(g, 2, slot(g, x, c, y), sib)

    def relay(g):
        gwait(g, 0, slot(g, xo, c, y))
        gsend(g, 3, slot(g, xo, c, y, 0), ynb)
        gsend(g, 5, slot(g, xo, c, y), sib)
        gwait(g, 1, slot(g, x, c, yo))
        gsend(g, 4, slot(g, x, c, yo, 1), xnb)
        gsend(g, 6, slot(g, x, c, yo), sib)

    def relay_diag(g):
        for h in range(2):
            gwait(g, 3 + h, slot(g, xo, c, yo, h))
            gsend(g, 7 + h, slot(g, xo, c, yo, h), sib)

    def wait_sib(g):
        gwait(g, 2, slot(g, x, co, y))
        gwait(g, 5, slot(g, xo, co, y))
        gwait(g, 6, slot(g, x, co, yo))
        gwait(g, 7, slot(g, xo, co, yo, 0))
        gwait(g, 8, slot(g, xo, co, yo, 1))

    def base(g):
        sub3 = lax.broadcasted_iota(jnp.int32, (3, 8, 128), 1)
        lane3 = lanes((3, 8, 128))
        seg3 = lane3 >> 4
        seg24 = lanes((24, 128)) & 112
        here = [(sub3 == (lane3 & 7)) & (((lane3 >> 3) & 1) == xr) for xr in range(2)]
        segs = [seg3 == lb for lb in range(8)]
        low = [[None, None] for _ in range(4)]
        for nb in range(4):
            xr, qr = nb // 2, nb % 2
            for qc in range(2):
                acc = dg[g, :, qc, qr, 0, xr]
                for lb in range(1, 8):
                    acc = jnp.where(segs[lb], dg[g, :, qc, qr, lb, xr], acc)
                low[nb][qc] = acc
        rec = []
        for qc in range(2):
            dsum = jnp.where(here[0], low[qc][qc], 0.0) + jnp.where(here[1], low[2 + qc][qc], 0.0)
            rec.append(1.0 / jnp.sum(dsum, axis=1, keepdims=True))
        rhs = []
        for nb in range(4):
            for qc in range(2):
                low[nb][qc] = (low[nb][qc] * rec[qc]).reshape(24, 128)
            rhs.append([jnp.where(here[nb // 2], 1.0, 0.0) if nb % 2 == qc else jnp.zeros((3, 8, 128), F32)
                        for qc in range(2)])
        below = [sub3 > ek for ek in range(7)]
        for k in range(32):
            nk, ek = k // 8, k % 8
            xk, qk = nk // 2, nk % 2
            idx = seg24 + (8 * xk + ek)
            pivot = [rhs[nk][qc][:, ek:ek + 1, :] for qc in range(2)]
            for nb in range(nk, 4):
                if nb == nk and ek == 7:
                    continue
                col = along(low[nb][qk], idx).reshape(3, 8, 128)
                if nb == nk:
                    col = jnp.where(below[ek], col, 0.0)
                for qc in range(2):
                    rhs[nb][qc] = rhs[nb][qc] - col * pivot[qc]
        for nb in range(4):
            xr, qr = nb // 2, nb % 2
            idx = (seg3 * 16 + 8 * xr + sub3).reshape(24, 128)
            scale = along(jnp.broadcast_to(rec[qr], (3, 8, 128)).reshape(24, 128), idx).reshape(3, 8, 128)
            for qc in range(2):
                val = rhs[nb][qc] * scale
                for lb in range(8):
                    inv[g, :, qc, qr, lb, xr] = jnp.where(segs[lb], val, 0.0)

    def both(ref_of):
        return jnp.concatenate([ref_of(0), ref_of(1)], axis=1)

    def inv_full(b):
        return both(lambda qc: inv[(*DIAG_AT[b], qc)].reshape(256, 128))

    def low_block(k, j):
        return both(lambda qc: goff[OFF_AT[k, j], qc].reshape(256, 128))

    def rows_of(tiles):
        return jnp.concatenate(tiles, axis=0)

    def double(blocks, w):
        pairs = range(4 // w)
        shape = (2, w, 2, 8, 128)
        half = lanes(shape) >> {1: 4, 2: 5, 4: 6}[w]
        even = [half == 2 * p for p in pairs]
        zero = jnp.zeros(shape, F32)
        odd_rows = [pl.ds((2 * p + 1) * w, w) for p in pairs]
        temps = []
        for b in blocks:
            at = DIAG_AT[b]

            def left(qc):
                acc = zero
                for p in pairs:
                    acc = jnp.where(even[p], dg[(*at, qc, slice(None), odd_rows[p])], acc)
                return acc.reshape(32 * w, 128)
            temps.append(hdot(both(left), inv_full(b)))
        for b, temp in zip(blocks, temps):
            at = DIAG_AT[b]

            def left(qc):
                acc = inv[(*at, qc, slice(None), odd_rows[0])]
                for p in pairs[1:]:
                    acc = acc + inv[(*at, qc, slice(None), odd_rows[p])]
                return acc.reshape(32 * w, 128)

            def right(qc):
                mine = temp[:, 128 * qc:128 * qc + 128].reshape(shape)
                parts = []
                for p in pairs:
                    parts += [zero, jnp.where(even[p], mine, 0.0)]
                return jnp.concatenate(parts, axis=1).reshape(256, 128)
            prod = -hdot(both(left), both(right))
            for qc in range(2):
                piece = prod[:, 128 * qc:128 * qc + 128].reshape(shape)
                for p in pairs:
                    ref = (*at, qc, slice(None), odd_rows[p])
                    inv[ref] = jnp.where(even[p], piece, inv[ref])

    def diag_inverses(g):
        unpack(g)
        base(g)
        for w in (1, 2, 4):
            double(DIAG[g], w)

    zst = [None] * 6

    def z_diag(j):
        return both(lambda qc: inv[(*DIAG_AT[j], qc, c, slice(None), x)].reshape(64, 128))

    def emit(i, j, blk):
        out[64 * i:64 * i + 64, 128 * j:128 * j + 128] = blk

    def add_terms(j, ks, acc):
        for k in ks:
            prod = hdot(zst[k], low_block(k, j))
            for i in range(k, 6):
                part = prod[64 * (i - k):64 * (i - k) + 64]
                acc[i] = part if acc[i] is None else acc[i] + part

    def finish(j, acc):
        emit(j, j, inv[(*DIAG_AT[j], y, c, slice(None), x)].reshape(64, 128))
        if j == 5:
            zst[5] = z_diag(5)
            return
        terms = rows_of(acc[j + 1:])
        if j == 0:
            res = -hdot(terms, inv[(*DIAG_AT[0], y)].reshape(256, 128))
            for i in range(1, 6):
                emit(i, 0, res[64 * (i - 1):64 * i])
            return
        res = -hdot(terms, inv_full(j))
        zst[j] = rows_of([z_diag(j), res])
        mine = jnp.where(y == 0, res[:, 0:128], res[:, 128:256])
        for i in range(j + 1, 6):
            emit(i, j, mine[64 * (i - j - 1):64 * (i - j)])

    pack(D1)
    pl.semaphore_wait(barrier, 3)
    own(D1)
    pack(D2)
    own(D2)
    own(O1)
    for i in range(6):
        if i < 5:
            out[64 * i:64 * i + 64, 128 * (i + 1):768] = jnp.zeros((64, 128 * (5 - i)), F32)
    relay(D1)
    own(O2)
    relay(D2)
    own(O3)
    relay(O1)
    own(O4)
    relay_diag(D1)
    wait_sib(D1)
    relay(O2)
    own(O5)
    relay_diag(D2)
    diag_inverses(D1)
    relay(O3)
    relay_diag(O1)
    wait_sib(D2)
    diag_inverses(D2)
    relay(O4)
    relay_diag(O2)
    wait_sib(O1)
    finish(5, None)
    acc = [None] * 6
    add_terms(4, (5,), acc)
    finish(4, acc)
    acc = [None] * 6
    add_terms(3, (5, 4), acc)
    finish(3, acc)
    relay(O5)
    relay_diag(O3)
    wait_sib(O2)
    acc = [None] * 6
    add_terms(2, (5, 4, 3), acc)
    finish(2, acc)
    relay_diag(O4)
    wait_sib(O3)
    acc = [None] * 6
    add_terms(1, (5, 4, 3), acc)
    relay_diag(O5)
    wait_sib(O4)
    add_terms(1, (2,), acc)
    finish(1, acc)
    acc = [None] * 6
    add_terms(0, (5, 4), acc)
    wait_sib(O5)
    add_terms(0, (3, 2, 1), acc)
    finish(0, acc)

    for cp in sends:
        cp.wait_send()


def solution(mesh):
    spec = P(("batch", "row"), "col")

    def body(local_l):
        rows, cols = local_l.shape
        return pl.pallas_call(
            kernel,
            out_shape=jax.ShapeDtypeStruct((rows, cols), F32),
            in_specs=[pl.BlockSpec(memory_space=pl.ANY)],
            out_specs=pl.BlockSpec(memory_space=pltpu.VMEM),
            scratch_shapes=[
                pltpu.VMEM((6, 8, 8, 128), F32),
                pltpu.VMEM((2, 2, 2, 2, 15, 8, 128), F32),
                pltpu.VMEM((2, 3, 2, 2, 8, 2, 8, 128), F32),
                pltpu.VMEM((15, 2, 2, 8, 2, 8, 128), F32),
                pltpu.VMEM((2, 3, 2, 2, 8, 2, 8, 128), F32),
                pltpu.SemaphoreType.DMA((21,)),
                pltpu.SemaphoreType.DMA((7, 9)),
                pltpu.SemaphoreType.DMA((7, 9)),
            ],
            compiler_params=pltpu.CompilerParams(
                collective_id=0, has_side_effects=True, vmem_limit_bytes=60 * 1024 * 1024),
        )(local_l.reshape(rows // 8, 8, cols))

    return jax.shard_map(body, mesh=mesh, in_specs=(spec,), out_specs=spec, check_vma=False)
```

time: 428 us -> 34 us (0.08)
  other arithmetic: 161 us -> 0 us
  blocking collectives: 98.1 us -> 0 us
  local copies, waits for them, and re-layouts: 93.9 us -> 2.36 us
  waiting for transfers between devices: 46.2 us -> 0 us
  Pallas kernels: 0 us -> 31.5 us
  between operations: 13.6 us -> 0.01 us
  matrix products: 11.7 us -> 0 us
    another operation x10 -> x0, other arithmetic: 159 us -> none  [the longest x8 158 us: leaf_inverses(): lax.linalg.triangular_solve(natural, rhs_batch, left_side=True, lower=True)]
    all_gather x11 -> x0, blocking collectives: 98.1 us -> none  [the longest x6 45 us: cyclic_product(): left_panel = natural_inner_cols(lax.all_gather(left, 'col', axis=2))]
    reshape x11 -> x0, local copies, waits for them, and re-layouts: 50.5 us -> none  [the longest x1 25.2 us: leaf_inverses(): split_view.transpose(0, 2, 1, 3, 5, 4, 6)]
    all_gather x3 -> x0, waiting for transfers between devices: 46.2 us -> none  [the longest x1 35.6 us: leaf_inverses(): lax.all_gather(lax.all_gather(diag_blocks, 'row', axis=1), 'col', axis=3)]
    pallas_call x0 -> x1, Pallas kernels: none -> 31.5 us  [body(): pl.pallas_call(kernel, out_shape=jax.ShapeDtypeStruct((rows, cols), F32),...]
    transpose x9 -> x0, local copies, waits for them, and re-layouts: 29.1 us -> none  [the longest x1 27.3 us: leaf_inverses(): split_view.transpose(0, 2, 1, 3, 5, 4, 6)]
    dot_general x6 -> x0, matrix products: 7.27 us -> none  [highest_matmul(): jnp.einsum('sik,skj->sij', left, right, precision=lax.Precision.HIGHEST,...]
    all_gather x8 -> x0, local copies, waits for them, and re-layouts: 5.81 us -> none  [the longest x1 2.87 us: leaf_inverses(): lax.all_gather(lax.all_gather(diag_blocks, 'row', axis=1), 'col', axis=3)]
  transfers between devices with their start and end apart: 4 -> 0, of which waited for: 3 -> 0; matrix products, arithmetic and copies ran while one was open for 2% -> 0% of each run, Pallas kernels for 0% -> 0%
where the time goes in v2:
time: 34 us; the launch traced here: 33.8 us
  Pallas kernels  31.5 us (93%)
  local copies, waits for them, and re-layouts  2.36 us (7%)
    pallas_call x1, Pallas kernels, body(): pl.pallas_call(kernel, out_shape=jax.ShapeDtypeStruct((rows, cols), F32),...  31.5 us
    unnamed x1, local copies, waits for them, and re-layouts  2.36 us

profile of v2, /device:TPU:0, one launch (start us, length us, event | category | flops | bytes accessed | tf_op | source)
XLA Modules:
  0.0 33.8 jit_solution(12141309252980550239)
XLA Ops:
  0.0 31.5 %shard_map.17 = f32[384,768]{1,0:T(8,128)} custom-call(f32[48,8,768]{2,1,0:T(8,128)} %bitcast.1), custom_call_target="tpu_custom_call" | custom-call | tf_op jit(solution)/shard_map/pallas_call | solution.py:334
  31.5 2.4 %copy.3 = f32[384,768]{1,0:T(8,128)} copy(f32[384,768]{1,0:T(8,128)} %shard_map.17) | data formatting | bytes 2359296

commit v3 on v2

v3 whole, which is shorter than its diff:
```python
import jax
import jax.numpy as jnp
from jax import lax
from jax.experimental import pallas as pl
from jax.experimental.pallas import tpu as pltpu
from jax.sharding import PartitionSpec as P

MESH = pl.DeviceIdType.MESH
F32 = jnp.float32
OFF = (
    ((5, 4), (4, 3), (5, 3)),
    ((3, 2), (4, 2), (5, 2)),
    ((2, 1), (3, 1), (4, 1), (5, 1)),
    ((1, 0), (2, 0)),
    ((3, 0), (4, 0)),
    ((5, 0),),
)
DG, O1, O2, O3, O4, O5, O6 = range(7)
OFF_LIST = [blk for grp in OFF for blk in grp]
OFF_AT = {blk: n for n, blk in enumerate(OFF_LIST)}
START = [OFF_AT[grp[0]] for grp in OFF]


def hdot(left, right):
    return jnp.dot(left, right, precision=lax.Precision.HIGHEST, preferred_element_type=F32)


def kernel(inp, out, raw, dpk, dg, goff, inv, loc_sem, g_send, g_recv):
    row = lax.axis_index("row")
    y = lax.axis_index("col")
    x = row // 2
    c = row % 2
    xo, yo, co = 1 - x, 1 - y, 1 - c
    sib = {"row": 2 * x + co}
    xnb = {"row": 2 * xo + c}
    ynb = {"col": yo}

    def take(bi, bj, dst, sem):
        return pltpu.make_async_copy(inp.at[pl.ds(8 * bi, 8), :, pl.ds(128 * bj, 128)], dst, sem)

    local = [[take(b, b, raw.at[b], loc_sem.at[b]) for b in range(6)]]
    for grp in OFF:
        local.append([take(bi, bj, goff.at[OFF_AT[bi, bj], y, c, :, x], loc_sem.at[6 + OFF_AT[bi, bj]])
                      for bi, bj in grp])
    for grp in local:
        for cp in grp:
            cp.start()

    barrier = pltpu.get_barrier_semaphore()
    for nbr in (sib, xnb, ynb):
        pl.semaphore_signal(barrier, inc=1, device_id=nbr, device_id_type=MESH)

    sub = lax.broadcasted_iota(jnp.int32, (8, 128), 0)
    lane = lax.broadcasted_iota(jnp.int32, (8, 128), 1)

    def lanes(shape):
        return lax.broadcasted_iota(jnp.int32, shape, len(shape) - 1)

    def along(tile, idx):
        return jnp.take_along_axis(tile, idx, axis=1, mode="promise_in_bounds")

    def turn(tile, n):
        return along(tile, (lanes(tile.shape) + (128 - n)) & 127)

    def pack():
        for b in range(6):
            local[DG][b].wait()
            dpk[y, c, x, 5 * b] = raw[b, 7]
            for p in range(3):
                n = 112 - 16 * p
                dpk[y, c, x, 5 * b + 1 + p] = jnp.where(lane < n, raw[b, 6 - p], turn(raw[b, p], n))
            dpk[y, c, x, 5 * b + 4] = raw[b, 3]

    def unpack():
        for b in range(6):
            for qc in range(2):
                for lb in range(8):
                    if lb >= 3:
                        tiles = dpk[qc, :, :, 5 * b + 7 - lb]
                    else:
                        tiles = dpk[qc, :, :, 5 * b + 1 + lb].reshape(32, 128)
                        tiles = turn(tiles, 16 * (lb + 1)).reshape(2, 2, 8, 128)
                    dg[b, qc, :, lb] = tiles

    def slot(g, sx, sc, sy, half=None):
        if g == DG:
            lo, num = (0, 30) if half is None else (15 * half, 15)
            return dpk.at[sy, sc, sx, pl.ds(lo, num)]
        lo, num = (0, 8) if half is None else (4 * half, 4)
        return goff.at[pl.ds(START[g - 1], len(OFF[g - 1])), sy, sc, pl.ds(lo, num), sx]

    sends = []

    def gsend(g, k, ref, dev):
        cp = pltpu.make_async_remote_copy(ref, ref, g_send.at[g, k], g_recv.at[g, k], device_id=dev, device_id_type=MESH)
        cp.start()
        sends.append(cp)

    def gwait(g, k, ref):
        pltpu.make_async_remote_copy(ref, ref, g_send.at[g, k], g_recv.at[g, k], device_id=sib,
                                     device_id_type=MESH).wait_recv()

    def own(g):
        if g != DG:
            for cp in local[g]:
                cp.wait()
        gsend(g, 0, slot(g, x, c, y), xnb)
        gsend(g, 1, slot(g, x, c, y), ynb)
        gsend(g, 2, slot(g, x, c, y), sib)

    def relay(g):
        gwait(g, 0, slot(g, xo, c, y))
        gsend(g, 3, slot(g, xo, c, y, 0), ynb)
        gsend(g, 5, slot(g, xo, c, y), sib)
        gwait(g, 1, slot(g, x, c, yo))
        gsend(g, 4, slot(g, x, c, yo, 1), xnb)
        gsend(g, 6, slot(g, x, c, yo), sib)

    def relay_diag(g):
        for h in range(2):
            gwait(g, 3 + h, slot(g, xo, c, yo, h))
            gsend(g, 7 + h, slot(g, xo, c, yo, h), sib)

    def wait_sib(g):
        gwait(g, 2, slot(g, x, co, y))
        gwait(g, 5, slot(g, xo, co, y))
        gwait(g, 6, slot(g, x, co, yo))
        gwait(g, 7, slot(g, xo, co, yo, 0))
        gwait(g, 8, slot(g, xo, co, yo, 1))

    def base(at):
        sub3 = lax.broadcasted_iota(jnp.int32, (3, 8, 128), 1)
        lane3 = lanes((3, 8, 128))
        seg3 = lane3 >> 4
        seg24 = lanes((24, 128)) & 112
        here = [(sub3 == (lane3 & 7)) & (((lane3 >> 3) & 1) == xr) for xr in range(2)]
        segs = [seg3 == lb for lb in range(8)]
        low = [[None, None] for _ in range(4)]
        for nb in range(4):
            xr, qr = nb // 2, nb % 2
            for qc in range(2):
                acc = dg[at:at + 3, qc, qr, 0, xr]
                for lb in range(1, 8):
                    acc = jnp.where(segs[lb], dg[at:at + 3, qc, qr, lb, xr], acc)
                low[nb][qc] = acc
        rec = []
        for qc in range(2):
            dsum = jnp.where(here[0], low[qc][qc], 0.0) + jnp.where(here[1], low[2 + qc][qc], 0.0)
            rec.append(1.0 / jnp.sum(dsum, axis=1, keepdims=True))
        rhs = []
        for nb in range(4):
            for qc in range(2):
                low[nb][qc] = (low[nb][qc] * rec[qc]).reshape(24, 128)
            rhs.append([jnp.where(here[nb // 2], 1.0, 0.0) if nb % 2 == qc else jnp.zeros((3, 8, 128), F32)
                        for qc in range(2)])
        below = [sub3 > ek for ek in range(7)]
        for k in range(32):
            nk, ek = k // 8, k % 8
            xk, qk = nk // 2, nk % 2
            idx = seg24 + (8 * xk + ek)
            pivot = [rhs[nk][qc][:, ek:ek + 1, :] for qc in range(2)]
            for nb in range(nk, 4):
                if nb == nk and ek == 7:
                    continue
                col = along(low[nb][qk], idx).reshape(3, 8, 128)
                if nb == nk:
                    col = jnp.where(below[ek], col, 0.0)
                for qc in range(2):
                    rhs[nb][qc] = rhs[nb][qc] - col * pivot[qc]
        for nb in range(4):
            xr, qr = nb // 2, nb % 2
            idx = (seg3 * 16 + 8 * xr + sub3).reshape(24, 128)
            scale = along(jnp.broadcast_to(rec[qr], (3, 8, 128)).reshape(24, 128), idx).reshape(3, 8, 128)
            for qc in range(2):
                val = rhs[nb][qc] * scale
                for lb in range(8):
                    inv[at:at + 3, qc, qr, lb, xr] = jnp.where(segs[lb], val, 0.0)

    def both(ref_of):
        return jnp.concatenate([ref_of(0), ref_of(1)], axis=1)

    def inv_full(b):
        return both(lambda qc: inv[b, qc].reshape(256, 128))

    def low_block(k, j):
        return both(lambda qc: goff[OFF_AT[k, j], qc].reshape(256, 128))

    def rows_of(tiles):
        return jnp.concatenate(tiles, axis=0)

    def double(w):
        pairs = range(4 // w)
        n = 16 * w
        shift = {1: 4, 2: 5, 4: 6}[w]
        shape = (2, w, 2, 8, 128)
        part = lanes(shape) >> shift
        even = [part == 2 * p for p in pairs]
        pair = [(lanes((w, 2, 8, 128)) >> (shift + 1)) == p for p in pairs]
        zero = jnp.zeros(shape, F32)
        first = (lanes((n, 128)) & n) == 0
        hole = jnp.zeros((128, 128), F32)

        def rows(p, odd):
            return pl.ds((2 * p + odd) * w, w)

        def twin(one, two):
            return rows_of([both(lambda h: (one, hole)[h]), both(lambda h: (hole, two)[h])])

        def low_left(b):
            acc = [zero, zero]
            for qc in range(2):
                for p in pairs:
                    acc[qc] = jnp.where(even[p], dg[b, qc, :, rows(p, 1)], acc[qc])
            return acc[0].reshape(2 * n, 128) + turn(acc[1].reshape(2 * n, 128), n)

        def up_inv(b):
            parts = []
            for p in pairs:
                for q in range(2):
                    one, two = (inv[b, qc, q, rows(p, 0)].reshape(n, 128) for qc in range(2))
                    parts.append(jnp.where(first, one, turn(two, n)))
            return rows_of(parts)

        def low_inv(b):
            acc = [inv[b, qc, :, rows(0, 1)] for qc in range(2)]
            for qc in range(2):
                for p in pairs[1:]:
                    acc[qc] = acc[qc] + inv[b, qc, :, rows(p, 1)]
            return turn(acc[0].reshape(2 * n, 128), -n) + acc[1].reshape(2 * n, 128)

        def temp_rows(temp):
            temp = temp.reshape(shape)
            return rows_of([jnp.where(pair[p], temp[q], 0.0).reshape(n, 128) for p in pairs for q in range(2)])

        two_blocks = ((5, 4), (3, 2), (1, 0))
        temps = [hdot(both(lambda h: low_left(bs[h])), twin(up_inv(bs[0]), up_inv(bs[1]))) for bs in two_blocks]
        for bs, temp in zip(two_blocks, temps):
            prod = -hdot(both(lambda h: low_inv(bs[h])), twin(temp_rows(temp[:, 0:128]), temp_rows(temp[:, 128:256])))
            for h, b in enumerate(bs):
                piece = prod[:, 128 * h:128 * h + 128]
                for qc, val in enumerate((piece, turn(piece, -n))):
                    val = val.reshape(shape)
                    for p in pairs:
                        inv[b, qc, :, rows(p, 1)] = jnp.where(even[p], val, inv[b, qc, :, rows(p, 1)])

    zst = [None] * 6

    def z_diag(j):
        return both(lambda qc: inv[j, qc, c, :, x].reshape(64, 128))

    def emit(i, j, blk):
        out[64 * i:64 * i + 64, 128 * j:128 * j + 128] = blk

    def add_terms(j, ks, acc):
        for k in ks:
            prod = hdot(zst[k], low_block(k, j))
            for i in range(k, 6):
                part = prod[64 * (i - k):64 * (i - k) + 64]
                acc[i] = part if acc[i] is None else acc[i] + part

    def finish(j, acc):
        emit(j, j, inv[j, y, c, :, x].reshape(64, 128))
        if j == 5:
            zst[5] = z_diag(5)
            return
        res = -hdot(rows_of(acc[j + 1:]), inv_full(j))
        zst[j] = rows_of([z_diag(j), res])
        mine = jnp.where(y == 0, res[:, 0:128], res[:, 128:256])
        for i in range(j + 1, 6):
            emit(i, j, mine[64 * (i - j - 1):64 * (i - j)])

    def finish_first(acc, lo, hi):
        res = -hdot(rows_of(acc[lo:hi]), inv[0, y].reshape(256, 128))
        for i in range(lo, hi):
            emit(i, 0, res[64 * (i - lo):64 * (i - lo) + 64])

    pack()
    pl.semaphore_wait(barrier, 3)
    own(DG)
    own(O1)
    for i in range(5):
        out[64 * i:64 * i + 64, 128 * (i + 1):768] = jnp.zeros((64, 128 * (5 - i)), F32)
    relay(DG)
    own(O2)
    relay(O1)
    own(O3)
    relay_diag(DG)
    wait_sib(DG)
    unpack()
    base(0)
    base(3)
    relay(O2)
    own(O4)
    double(1)
    double(2)
    relay_diag(O1)
    double(4)
    relay(O3)
    own(O5)
    own(O6)
    wait_sib(O1)
    finish(5, None)
    acc = [None] * 6
    add_terms(4, (5,), acc)
    finish(4, acc)
    acc = [None] * 6
    add_terms(3, (5, 4), acc)
    finish(3, acc)
    relay_diag(O2)
    wait_sib(O2)
    acc = [None] * 6
    add_terms(2, (5, 4, 3), acc)
    finish(2, acc)
    relay(O4)
    relay_diag(O3)
    wait_sib(O3)
    acc = [None] * 6
    add_terms(1, (5, 4, 3, 2), acc)
    finish(1, acc)
    emit(0, 0, inv[0, y, c, :, x].reshape(64, 128))
    relay(O5)
    relay(O6)
    relay_diag(O4)
    wait_sib(O4)
    acc = [None] * 6
    add_terms(0, (1, 2), acc)
    relay_diag(O5)
    relay_diag(O6)
    wait_sib(O5)
    add_terms(0, (3, 4), acc)
    finish_first(acc, 1, 5)
    wait_sib(O6)
    add_terms(0, (5,), acc)
    finish_first(acc, 5, 6)

    for cp in sends:
        cp.wait_send()


def solution(mesh):
    spec = P(("batch", "row"), "col")

    def body(local_l):
        rows, cols = local_l.shape
        return pl.pallas_call(
            kernel,
            out_shape=jax.ShapeDtypeStruct((rows, cols), F32),
            in_specs=[pl.BlockSpec(memory_space=pltpu.HBM)],
            out_specs=pl.BlockSpec(memory_space=pltpu.VMEM),
            scratch_shapes=[
                pltpu.VMEM((6, 8, 8, 128), F32),
                pltpu.VMEM((2, 2, 2, 30, 8, 128), F32),
                pltpu.VMEM((6, 2, 2, 8, 2, 8, 128), F32),
                pltpu.VMEM((15, 2, 2, 8, 2, 8, 128), F32),
                pltpu.VMEM((6, 2, 2, 8, 2, 8, 128), F32),
                pltpu.SemaphoreType.DMA((21,)),
                pltpu.SemaphoreType.DMA((7, 9)),
                pltpu.SemaphoreType.DMA((7, 9)),
            ],
            compiler_params=pltpu.CompilerParams(
                collective_id=0, has_side_effects=True, vmem_limit_bytes=40 * 1024 * 1024),
        )(pltpu.with_memory_space_constraint(local_l.reshape(rows // 8, 8, cols), pltpu.HBM))

    return jax.shard_map(body, mesh=mesh, in_specs=(spec,), out_specs=spec, check_vma=False)
```

time: 34 us -> 32.7 us (0.962)
  local copies, waits for them, and re-layouts: 2.36 us -> 1.02 us
    unnamed x1, local copies, waits for them, and re-layouts: 2.36 us -> 1.02 us
where the time goes in v3:
time: 32.7 us; the launch traced here: 32.3 us
  Pallas kernels  31.3 us (96%)
  local copies, waits for them, and re-layouts  1.02 us (3%)
    pallas_call x1, Pallas kernels, body(): pl.pallas_call(kernel, out_shape=jax.ShapeDtypeStruct((rows, cols), F32),...  31.3 us
    unnamed x1, local copies, waits for them, and re-layouts  1.02 us

profile of v3, /device:TPU:0, one launch (start us, length us, event | category | flops | bytes accessed | tf_op | source)
XLA Modules:
  0.0 32.3 jit_solution(7284470589671175399)
XLA Ops:
  0.0 31.3 %shard_map.17 = f32[384,768]{1,0:T(8,128)S(1)} custom-call(f32[48,8,768]{2,1,0:T(8,128)} %bitcast.1), custom_call_target="tpu_custom_call" | custom-call | tf_op jit(solution)/shard_map/pallas_call | solution.py:345
  31.3 1.0 %copy.3 = f32[384,768]{1,0:T(8,128)} copy(f32[384,768]{1,0:T(8,128)S(1)} %shard_map.17) | data formatting | bytes 2359296

commit v4 on v3

--- a/solution.py
+++ b/solution.py
@@ -8,14 +8,15 @@
 MESH = pl.DeviceIdType.MESH
 F32 = jnp.float32
 OFF = (
-    ((5, 4), (4, 3), (5, 3)),
+    ((5, 4),),
+    ((4, 3), (5, 3)),
     ((3, 2), (4, 2), (5, 2)),
     ((2, 1), (3, 1), (4, 1), (5, 1)),
     ((1, 0), (2, 0)),
     ((3, 0), (4, 0)),
     ((5, 0),),
 )
-DG, O1, O2, O3, O4, O5, O6 = range(7)
+DG, O1, O2, O3, O4, O5, O6, O7 = range(8)
 OFF_LIST = [blk for grp in OFF for blk in grp]
 OFF_AT = {blk: n for n, blk in enumerate(OFF_LIST)}
 START = [OFF_AT[grp[0]] for grp in OFF]
@@ -42,8 +43,8 @@
     for grp in OFF:
         local.append([take(bi, bj, goff.at[OFF_AT[bi, bj], y, c, :, x], loc_sem.at[6 + OFF_AT[bi, bj]])
                       for bi, bj in grp])
-    for grp in local:
-        for cp in grp:
+    for g in (O1, DG, O2, O3, O4, O5, O6, O7):
+        for cp in local[g]:
             cp.start()
 
     barrier = pltpu.get_barrier_semaphore()
@@ -65,6 +66,7 @@
     def pack():
         for b in range(6):
             local[DG][b].wait()
+        for b in range(6):
             dpk[y, c, x, 5 * b] = raw[b, 7]
             for p in range(3):
                 n = 112 - 16 * p
@@ -274,62 +276,67 @@
         for i in range(lo, hi):
             emit(i, 0, res[64 * (i - lo):64 * (i - lo) + 64])
 
+    pl.semaphore_wait(barrier, 3)
+    own(O1)
     pack()
-    pl.semaphore_wait(barrier, 3)
     own(DG)
-    own(O1)
+    own(O2)
     for i in range(5):
         out[64 * i:64 * i + 64, 128 * (i + 1):768] = jnp.zeros((64, 128 * (5 - i)), F32)
+    relay(O1)
     relay(DG)
-    own(O2)
-    relay(O1)
     own(O3)
+    relay(O2)
+    own(O4)
+    relay_diag(O1)
     relay_diag(DG)
     wait_sib(DG)
     unpack()
     base(0)
     base(3)
-    relay(O2)
-    own(O4)
+    relay(O3)
+    own(O5)
     double(1)
     double(2)
-    relay_diag(O1)
+    relay_diag(O2)
     double(4)
-    relay(O3)
-    own(O5)
-    own(O6)
     wait_sib(O1)
     finish(5, None)
     acc = [None] * 6
     add_terms(4, (5,), acc)
     finish(4, acc)
+    relay(O4)
+    own(O6)
+    own(O7)
+    wait_sib(O2)
     acc = [None] * 6
     add_terms(3, (5, 4), acc)
     finish(3, acc)
-    relay_diag(O2)
-    wait_sib(O2)
+    relay_diag(O3)
+    relay(O5)
+    wait_sib(O3)
     acc = [None] * 6
     add_terms(2, (5, 4, 3), acc)
     finish(2, acc)
-    relay(O4)
-    relay_diag(O3)
-    wait_sib(O3)
-    acc = [None] * 6
-    add_terms(1, (5, 4, 3, 2), acc)
+    emit(0, 0, inv[0, y, c, :, x].reshape(64, 128))
+    relay_diag(O4)
+    relay(O6)
+    wait_sib(O4)
+    acc = [None] * 6
+    add_terms(1, (5, 4), acc)
+    relay(O7)
+    add_terms(1, (3, 2), acc)
+    relay_diag(O5)
     finish(1, acc)
-    emit(0, 0, inv[0, y, c, :, x].reshape(64, 128))
-    relay(O5)
-    relay(O6)
-    relay_diag(O4)
-    wait_sib(O4)
+    relay_diag(O6)
+    relay_diag(O7)
+    wait_sib(O5)
     acc = [None] * 6
     add_terms(0, (1, 2), acc)
-    relay_diag(O5)
-    relay_diag(O6)
-    wait_sib(O5)
+    wait_sib(O6)
     add_terms(0, (3, 4), acc)
     finish_first(acc, 1, 5)
-    wait_sib(O6)
+    wait_sib(O7)
     add_terms(0, (5,), acc)
     finish_first(acc, 5, 6)
 
@@ -354,8 +361,8 @@
                 pltpu.VMEM((15, 2, 2, 8, 2, 8, 128), F32),
                 pltpu.VMEM((6, 2, 2, 8, 2, 8, 128), F32),
                 pltpu.SemaphoreType.DMA((21,)),
-                pltpu.SemaphoreType.DMA((7, 9)),
-                pltpu.SemaphoreType.DMA((7, 9)),
+                pltpu.SemaphoreType.DMA((8, 9)),
+                pltpu.SemaphoreType.DMA((8, 9)),
             ],
             compiler_params=pltpu.CompilerParams(
                 collective_id=0, has_side_effects=True, vmem_limit_bytes=40 * 1024 * 1024),

time: 32.7 us -> 33.1 us (1.012)
  Pallas kernels: 31.3 us -> 31.9 us
    pallas_call x1, Pallas kernels: 31.3 us -> 31.9 us  [body(): pl.pallas_call(kernel, out_shape=jax.ShapeDtypeStruct((rows, cols), F32),...]
where the time goes in v4:
time: 33.1 us; the launch traced here: 33 us
  Pallas kernels  31.9 us (96%)
  local copies, waits for them, and re-layouts  1.02 us (3%)
    pallas_call x1, Pallas kernels, body(): pl.pallas_call(kernel, out_shape=jax.ShapeDtypeStruct((rows, cols), F32),...  31.9 us
    unnamed x1, local copies, waits for them, and re-layouts  1.02 us

profile of v4, /device:TPU:0, one launch (start us, length us, event | category | flops | bytes accessed | tf_op | source)
XLA Modules:
  0.0 33.0 jit_solution(8732202510824621248)
XLA Ops:
  0.0 31.9 %shard_map.17 = f32[384,768]{1,0:T(8,128)S(1)} custom-call(f32[48,8,768]{2,1,0:T(8,128)} %bitcast.1), custom_call_target="tpu_custom_call" | custom-call | tf_op jit(solution)/shard_map/pallas_call | solution.py:352
  32.0 1.0 %copy.3 = f32[384,768]{1,0:T(8,128)} copy(f32[384,768]{1,0:T(8,128)S(1)} %shard_map.17) | data formatting | bytes 2359296

commit v5 on v3

--- a/solution.py
+++ b/solution.py
@@ -7,25 +7,17 @@
 
 MESH = pl.DeviceIdType.MESH
 F32 = jnp.float32
-OFF = (
-    ((5, 4), (4, 3), (5, 3)),
-    ((3, 2), (4, 2), (5, 2)),
-    ((2, 1), (3, 1), (4, 1), (5, 1)),
-    ((1, 0), (2, 0)),
-    ((3, 0), (4, 0)),
-    ((5, 0),),
-)
-DG, O1, O2, O3, O4, O5, O6 = range(7)
-OFF_LIST = [blk for grp in OFF for blk in grp]
-OFF_AT = {blk: n for n, blk in enumerate(OFF_LIST)}
-START = [OFF_AT[grp[0]] for grp in OFF]
+DB, DA, BO, AO = range(4)
+DIAG = {DB: (5, 4, 3), DA: (2, 1, 0)}
+OFF = {BO: ((5, 4), (4, 3), (5, 3)), AO: ((2, 1), (1, 0), (2, 0))}
+OFF_AT = {blk: 3 * (g - 2) + i for g, grp in OFF.items() for i, blk in enumerate(grp)}
 
 
 def hdot(left, right):
     return jnp.dot(left, right, precision=lax.Precision.HIGHEST, preferred_element_type=F32)
 
 
-def kernel(inp, out, raw, dpk, dg, goff, inv, loc_sem, g_send, g_recv):
+def kernel(inp, out, raw, dpk, dg, goff, cbuf, ubuf, inv, loc_sem, g_send, g_recv, c_send, c_recv, u_send, u_recv):
     row = lax.axis_index("row")
     y = lax.axis_index("col")
     x = row // 2
@@ -38,11 +30,11 @@
     def take(bi, bj, dst, sem):
         return pltpu.make_async_copy(inp.at[pl.ds(8 * bi, 8), :, pl.ds(128 * bj, 128)], dst, sem)
 
-    local = [[take(b, b, raw.at[b], loc_sem.at[b]) for b in range(6)]]
-    for grp in OFF:
-        local.append([take(bi, bj, goff.at[OFF_AT[bi, bj], y, c, :, x], loc_sem.at[6 + OFF_AT[bi, bj]])
-                      for bi, bj in grp])
-    for grp in local:
+    local = {g: [take(b, b, raw.at[b], loc_sem.at[b]) for b in DIAG[g]] for g in DIAG}
+    for g in OFF:
+        local[g] = [take(bi, bj, goff.at[OFF_AT[bi, bj], y, c, :, x], loc_sem.at[6 + OFF_AT[bi, bj]]) for bi, bj in OFF[g]]
+    local_c = [[take(3 + k, j, cbuf.at[j, k, c, :, x], loc_sem.at[12 + 3 * j + k]) for k in range(3)] for j in range(3)]
+    for grp in (local[DB], local[BO], local[DA], local_c[2], local_c[1], local_c[0], local[AO]):
         for cp in grp:
             cp.start()
 
@@ -62,71 +54,100 @@
     def turn(tile, n):
         return along(tile, (lanes(tile.shape) + (128 - n)) & 127)
 
-    def pack():
-        for b in range(6):
-            local[DG][b].wait()
-            dpk[y, c, x, 5 * b] = raw[b, 7]
+    def pack(g):
+        for cp in local[g]:
+            cp.wait()
+        for i, b in enumerate(DIAG[g]):
+            dpk[g, y, c, x, 5 * i] = raw[b, 7]
             for p in range(3):
                 n = 112 - 16 * p
-                dpk[y, c, x, 5 * b + 1 + p] = jnp.where(lane < n, raw[b, 6 - p], turn(raw[b, p], n))
-            dpk[y, c, x, 5 * b + 4] = raw[b, 3]
-
-    def unpack():
-        for b in range(6):
+                dpk[g, y, c, x, 5 * i + 1 + p] = jnp.where(lane < n, raw[b, 6 - p], turn(raw[b, p], n))
+            dpk[g, y, c, x, 5 * i + 4] = raw[b, 3]
+
+    def unpack(g):
+        for i, b in enumerate(DIAG[g]):
             for qc in range(2):
                 for lb in range(8):
                     if lb >= 3:
-                        tiles = dpk[qc, :, :, 5 * b + 7 - lb]
+                        tiles = dpk[g, qc, :, :, 5 * i + 7 - lb]
                     else:
-                        tiles = dpk[qc, :, :, 5 * b + 1 + lb].reshape(32, 128)
+                        tiles = dpk[g, qc, :, :, 5 * i + 1 + lb].reshape(32, 128)
                         tiles = turn(tiles, 16 * (lb + 1)).reshape(2, 2, 8, 128)
                     dg[b, qc, :, lb] = tiles
 
-    def slot(g, sx, sc, sy, half=None):
-        if g == DG:
-            lo, num = (0, 30) if half is None else (15 * half, 15)
-            return dpk.at[sy, sc, sx, pl.ds(lo, num)]
-        lo, num = (0, 8) if half is None else (4 * half, 4)
-        return goff.at[pl.ds(START[g - 1], len(OFF[g - 1])), sy, sc, pl.ds(lo, num), sx]
+    def slot(g, sx, sc, sy):
+        if g in DIAG:
+            return dpk.at[g, sy, sc, sx]
+        return goff.at[pl.ds(3 * (g - 2), 3), sy, sc, :, sx]
 
     sends = []
 
-    def gsend(g, k, ref, dev):
-        cp = pltpu.make_async_remote_copy(ref, ref, g_send.at[g, k], g_recv.at[g, k], device_id=dev, device_id_type=MESH)
+    def copy(ref, send, recv, dev):
+        return pltpu.make_async_remote_copy(ref, ref, send, recv, device_id=dev, device_id_type=MESH)
+
+    def start(cp):
         cp.start()
         sends.append(cp)
 
+    def gsend(g, k, ref, dev):
+        start(copy(ref, g_send.at[g, k], g_recv.at[g, k], dev))
+
     def gwait(g, k, ref):
-        pltpu.make_async_remote_copy(ref, ref, g_send.at[g, k], g_recv.at[g, k], device_id=sib,
-                                     device_id_type=MESH).wait_recv()
-
-    def own(g):
-        if g != DG:
-            for cp in local[g]:
-                cp.wait()
-        gsend(g, 0, slot(g, x, c, y), xnb)
-        gsend(g, 1, slot(g, x, c, y), ynb)
-        gsend(g, 2, slot(g, x, c, y), sib)
-
-    def relay(g):
+        copy(ref, g_send.at[g, k], g_recv.at[g, k], sib).wait_recv()
+
+    def own(g, to):
+        for k, dev in enumerate((xnb, ynb, sib)):
+            if "xys"[k] in to:
+                gsend(g, k, slot(g, x, c, y), dev)
+
+    def ready(g):
+        for cp in local[g]:
+            cp.wait()
+
+    def from_x(g):
         gwait(g, 0, slot(g, xo, c, y))
-        gsend(g, 3, slot(g, xo, c, y, 0), ynb)
-        gsend(g, 5, slot(g, xo, c, y), sib)
+        if g != AO:
+            gsend(g, 3, slot(g, xo, c, y), ynb)
+        gsend(g, 4, slot(g, xo, c, y), sib)
+
+    def from_y(g):
         gwait(g, 1, slot(g, x, c, yo))
-        gsend(g, 4, slot(g, x, c, yo, 1), xnb)
-        gsend(g, 6, slot(g, x, c, yo), sib)
-
-    def relay_diag(g):
-        for h in range(2):
-            gwait(g, 3 + h, slot(g, xo, c, yo, h))
-            gsend(g, 7 + h, slot(g, xo, c, yo, h), sib)
+        if g == AO:
+            gsend(g, 3, slot(g, x, c, yo), xnb)
+        gsend(g, 5, slot(g, x, c, yo), sib)
+
+    def from_diag(g):
+        gwait(g, 3, slot(g, xo, c, yo))
+        gsend(g, 6, slot(g, xo, c, yo), sib)
 
     def wait_sib(g):
         gwait(g, 2, slot(g, x, co, y))
-        gwait(g, 5, slot(g, xo, co, y))
-        gwait(g, 6, slot(g, x, co, yo))
-        gwait(g, 7, slot(g, xo, co, yo, 0))
-        gwait(g, 8, slot(g, xo, co, yo, 1))
+        gwait(g, 4, slot(g, xo, co, y))
+        gwait(g, 5, slot(g, x, co, yo))
+        gwait(g, 6, slot(g, xo, co, yo))
+
+    def c_slot(j, sx, sc):
+        return cbuf.at[j, :, sc, :, sx]
+
+    def c_own(j):
+        for cp in local_c[j]:
+            cp.wait()
+        for k, dev in enumerate((xnb, sib)):
+            start(copy(c_slot(j, x, c), c_send.at[j, k], c_recv.at[j, k], dev))
+
+    def c_relay(j):
+        copy(c_slot(j, xo, c), c_send.at[j, 0], c_recv.at[j, 0], sib).wait_recv()
+        start(copy(c_slot(j, xo, c), c_send.at[j, 2], c_recv.at[j, 2], sib))
+
+    def c_wait(j):
+        copy(c_slot(j, x, co), c_send.at[j, 1], c_recv.at[j, 1], sib).wait_recv()
+        copy(c_slot(j, xo, co), c_send.at[j, 2], c_recv.at[j, 2], sib).wait_recv()
+
+    def u_send_to(j):
+        start(copy(ubuf.at[j, y], u_send.at[j], u_recv.at[j], ynb))
+
+    def u_wait(j):
+        copy(ubuf.at[j, yo], u_send.at[j], u_recv.at[j], ynb).wait_recv()
 
     def base(at):
         sub3 = lax.broadcasted_iota(jnp.int32, (3, 8, 128), 1)
@@ -188,7 +209,7 @@
     def rows_of(tiles):
         return jnp.concatenate(tiles, axis=0)
 
-    def double(w):
+    def double(group, w):
         pairs = range(4 // w)
         n = 16 * w
         shift = {1: 4, 2: 5, 4: 6}[w]
@@ -232,10 +253,16 @@
             temp = temp.reshape(shape)
             return rows_of([jnp.where(pair[p], temp[q], 0.0).reshape(n, 128) for p in pairs for q in range(2)])
 
-        two_blocks = ((5, 4), (3, 2), (1, 0))
-        temps = [hdot(both(lambda h: low_left(bs[h])), twin(up_inv(bs[0]), up_inv(bs[1]))) for bs in two_blocks]
+        def product(lefts, rights):
+            if len(lefts) == 1:
+                return hdot(lefts[0], rights[0])
+            return hdot(jnp.concatenate(lefts, axis=1), twin(*rights))
+
+        two_blocks = (group[:2], group[2:])
+        temps = [product([low_left(b) for b in bs], [up_inv(b) for b in bs]) for bs in two_blocks]
         for bs, temp in zip(two_blocks, temps):
-            prod = -hdot(both(lambda h: low_inv(bs[h])), twin(temp_rows(temp[:, 0:128]), temp_rows(temp[:, 128:256])))
+            prod = -product([low_inv(b) for b in bs],
+                            [temp_rows(temp[:, 128 * h:128 * h + 128]) for h in range(len(bs))])
             for h, b in enumerate(bs):
                 piece = prod[:, 128 * h:128 * h + 128]
                 for qc, val in enumerate((piece, turn(piece, -n))):
@@ -274,31 +301,54 @@
         for i in range(lo, hi):
             emit(i, 0, res[64 * (i - lo):64 * (i - lo) + 64])
 
-    pack()
+    def inverses(g):
+        unpack(g)
+        base(min(DIAG[g]))
+        for w in (1, 2, 4):
+            double(DIAG[g], w)
+
+    def u_compute(j):
+        acc = [None] * 6
+        for k in (3, 4, 5):
+            prod = hdot(zst[k], cbuf[j, k - 3].reshape(256, 128))
+            for i in range(k, 6):
+                part = prod[64 * (i - k):64 * (i - k) + 64]
+                acc[i] = part if acc[i] is None else acc[i] + part
+        for i in (3, 4, 5):
+            ubuf[j, y, 64 * (i - 3):64 * (i - 3) + 64] = acc[i]
+
+    def u_add(j, acc):
+        for i in (3, 4, 5):
+            part = both(lambda q: ubuf[j, q, 64 * (i - 3):64 * (i - 3) + 64])
+            acc[i] = part if acc[i] is None else acc[i] + part
+
+    pack(DB)
     pl.semaphore_wait(barrier, 3)
-    own(DG)
-    own(O1)
+    own(DB, "xys")
+    ready(BO)
+    own(BO, "xys")
+    pack(DA)
+    own(DA, "xs")
+    c_own(2)
     for i in range(5):
         out[64 * i:64 * i + 64, 128 * (i + 1):768] = jnp.zeros((64, 128 * (5 - i)), F32)
-    relay(DG)
-    own(O2)
-    relay(O1)
-    own(O3)
-    relay_diag(DG)
-    wait_sib(DG)
-    unpack()
-    base(0)
-    base(3)
-    relay(O2)
-    own(O4)
-    double(1)
-    double(2)
-    relay_diag(O1)
-    double(4)
-    relay(O3)
-    own(O5)
-    own(O6)
-    wait_sib(O1)
+    from_x(DB)
+    from_y(DB)
+    c_own(1)
+    c_own(0)
+    from_x(BO)
+    own(DA, "y")
+    from_y(BO)
+    ready(AO)
+    own(AO, "xys")
+    from_x(DA)
+    from_diag(DB)
+    wait_sib(DB)
+    inverses(DB)
+    from_diag(BO)
+    c_relay(2)
+    from_y(DA)
+    wait_sib(BO)
     finish(5, None)
     acc = [None] * 6
     add_terms(4, (5,), acc)
@@ -306,32 +356,40 @@
     acc = [None] * 6
     add_terms(3, (5, 4), acc)
     finish(3, acc)
-    relay_diag(O2)
-    wait_sib(O2)
+    c_wait(2)
+    c_relay(1)
+    u_compute(2)
+    u_send_to(2)
+    c_wait(1)
+    from_y(AO)
+    u_compute(1)
+    u_send_to(1)
+    c_relay(0)
+    from_diag(DA)
+    c_wait(0)
+    u_compute(0)
+    u_send_to(0)
+    from_x(AO)
+    wait_sib(DA)
+    inverses(DA)
+    from_diag(AO)
+    emit(0, 0, inv[0, y, c, :, x].reshape(64, 128))
+    u_wait(2)
     acc = [None] * 6
-    add_terms(2, (5, 4, 3), acc)
+    u_add(2, acc)
     finish(2, acc)
-    relay(O4)
-    relay_diag(O3)
-    wait_sib(O3)
+    wait_sib(AO)
     acc = [None] * 6
-    add_terms(1, (5, 4, 3, 2), acc)
+    add_terms(1, (2,), acc)
+    u_wait(1)
+    u_add(1, acc)
     finish(1, acc)
-    emit(0, 0, inv[0, y, c, :, x].reshape(64, 128))
-    relay(O5)
-    relay(O6)
-    relay_diag(O4)
-    wait_sib(O4)
     acc = [None] * 6
-    add_terms(0, (1, 2), acc)
-    relay_diag(O5)
-    relay_diag(O6)
-    wait_sib(O5)
-    add_terms(0, (3, 4), acc)
-    finish_first(acc, 1, 5)
-    wait_sib(O6)
-    add_terms(0, (5,), acc)
-    finish_first(acc, 5, 6)
+    add_terms(0, (2, 1), acc)
+    finish_first(acc, 1, 3)
+    u_wait(0)
+    u_add(0, acc)
+    finish_first(acc, 3, 6)
 
     for cp in sends:
         cp.wait_send()
@@ -349,13 +407,19 @@
             out_specs=pl.BlockSpec(memory_space=pltpu.VMEM),
             scratch_shapes=[
                 pltpu.VMEM((6, 8, 8, 128), F32),
-                pltpu.VMEM((2, 2, 2, 30, 8, 128), F32),
+                pltpu.VMEM((2, 2, 2, 2, 15, 8, 128), F32),
                 pltpu.VMEM((6, 2, 2, 8, 2, 8, 128), F32),
-                pltpu.VMEM((15, 2, 2, 8, 2, 8, 128), F32),
+                pltpu.VMEM((6, 2, 2, 8, 2, 8, 128), F32),
+                pltpu.VMEM((3, 3, 2, 8, 2, 8, 128), F32),
+                pltpu.VMEM((3, 2, 192, 128), F32),
                 pltpu.VMEM((6, 2, 2, 8, 2, 8, 128), F32),
                 pltpu.SemaphoreType.DMA((21,)),
-                pltpu.SemaphoreType.DMA((7, 9)),
-                pltpu.SemaphoreType.DMA((7, 9)),
+                pltpu.SemaphoreType.DMA((4, 7)),
+                pltpu.SemaphoreType.DMA((4, 7)),
+                pltpu.SemaphoreType.DMA((3, 3)),
+                pltpu.SemaphoreType.DMA((3, 3)),
+                pltpu.SemaphoreType.DMA((3,)),
+                pltpu.SemaphoreType.DMA((3,)),
             ],
             compiler_params=pltpu.CompilerParams(
                 collective_id=0, has_side_effects=True, vmem_limit_bytes=40 * 1024 * 1024),

time: 32.7 us -> 29.6 us (0.905)
  Pallas kernels: 31.3 us -> 28.4 us
    pallas_call x1, Pallas kernels: 31.3 us -> 28.4 us  [body(): pl.pallas_call(kernel, out_shape=jax.ShapeDtypeStruct((rows, cols), F32),...]
where the time goes in v5:
time: 29.6 us; the launch traced here: 29.5 us
  Pallas kernels  28.4 us (96%)
  local copies, waits for them, and re-layouts  1.02 us (3%)
    pallas_call x1, Pallas kernels, body(): pl.pallas_call(kernel, out_shape=jax.ShapeDtypeStruct((rows, cols), F32),...  28.4 us
    unnamed x1, local copies, waits for them, and re-layouts  1.02 us

profile of v5, /device:TPU:0, one launch (start us, length us, event | category | flops | bytes accessed | tf_op | source)
XLA Modules:
  0.0 29.5 jit_solution(17575337104317816180)
XLA Ops:
  0.0 28.4 %shard_map.17 = f32[384,768]{1,0:T(8,128)S(1)} custom-call(f32[48,8,768]{2,1,0:T(8,128)} %bitcast.1), custom_call_target="tpu_custom_call" | custom-call | tf_op jit(solution)/shard_map/pallas_call | solution.py:403
  28.4 1.0 %copy.3 = f32[384,768]{1,0:T(8,128)} copy(f32[384,768]{1,0:T(8,128)S(1)} %shard_map.17) | data formatting | bytes 2359296

commit v6 on v5

--- a/solution.py
+++ b/solution.py
@@ -333,21 +333,27 @@
     for i in range(5):
         out[64 * i:64 * i + 64, 128 * (i + 1):768] = jnp.zeros((64, 128 * (5 - i)), F32)
     from_x(DB)
+    own(DA, "y")
     from_y(DB)
     c_own(1)
     c_own(0)
     from_x(BO)
-    own(DA, "y")
     from_y(BO)
+    from_x(DA)
     ready(AO)
     own(AO, "xys")
-    from_x(DA)
     from_diag(DB)
     wait_sib(DB)
-    inverses(DB)
+    unpack(DB)
+    base(3)
+    from_y(DA)
+    c_relay(2)
+    double(DIAG[DB], 1)
     from_diag(BO)
-    c_relay(2)
-    from_y(DA)
+    double(DIAG[DB], 2)
+    c_relay(1)
+    double(DIAG[DB], 4)
+    from_diag(DA)
     wait_sib(BO)
     finish(5, None)
     acc = [None] * 6
@@ -356,22 +362,24 @@
     acc = [None] * 6
     add_terms(3, (5, 4), acc)
     finish(3, acc)
+    c_relay(0)
+    wait_sib(DA)
     c_wait(2)
-    c_relay(1)
+    unpack(DA)
     u_compute(2)
+    base(0)
     u_send_to(2)
     c_wait(1)
+    u_compute(1)
+    double(DIAG[DA], 1)
+    u_send_to(1)
     from_y(AO)
-    u_compute(1)
-    u_send_to(1)
-    c_relay(0)
-    from_diag(DA)
     c_wait(0)
     u_compute(0)
+    double(DIAG[DA], 2)
     u_send_to(0)
     from_x(AO)
-    wait_sib(DA)
-    inverses(DA)
+    double(DIAG[DA], 4)
     from_diag(AO)
     emit(0, 0, inv[0, y, c, :, x].reshape(64, 128))
     u_wait(2)

time: 29.6 us -> 29.3 us (0.990)
  Pallas kernels: 28.4 us -> 28.1 us
    pallas_call x1, Pallas kernels: 28.4 us -> 28.1 us  [body(): pl.pallas_call(kernel, out_shape=jax.ShapeDtypeStruct((rows, cols), F32),...]
where the time goes in v6:
time: 29.3 us; the launch traced here: 29.1 us
  Pallas kernels  28.1 us (96%)
  local copies, waits for them, and re-layouts  1.02 us (3%)
    pallas_call x1, Pallas kernels, body(): pl.pallas_call(kernel, out_shape=jax.ShapeDtypeStruct((rows, cols), F32),...  28.1 us
    unnamed x1, local copies, waits for them, and re-layouts  1.02 us

profile of v6, /device:TPU:0, one launch (start us, length us, event | category | flops | bytes accessed | tf_op | source)
XLA Modules:
  0.0 29.1 jit_solution(14653948627670194570)
XLA Ops:
  0.0 28.1 %shard_map.17 = f32[384,768]{1,0:T(8,128)S(1)} custom-call(f32[48,8,768]{2,1,0:T(8,128)} %bitcast.1), custom_call_target="tpu_custom_call" | custom-call | tf_op jit(solution)/shard_map/pallas_call | solution.py:411
  28.1 1.0 %copy.3 = f32[384,768]{1,0:T(8,128)} copy(f32[384,768]{1,0:T(8,128)S(1)} %shard_map.17) | data formatting | bytes 2359296

commit v7 on v6

--- a/solution.py
+++ b/solution.py
@@ -13,11 +13,18 @@
 OFF_AT = {blk: 3 * (g - 2) + i for g, grp in OFF.items() for i, blk in enumerate(grp)}
 
 
+CGRP = [[(4, j), (5, j)] for j in range(3)] + [[(3, j) for j in range(3)]]
+
+
+def c_at(k, j):
+    return 6 + j if k == 3 else 2 * j + k - 4
+
+
 def hdot(left, right):
     return jnp.dot(left, right, precision=lax.Precision.HIGHEST, preferred_element_type=F32)
 
 
-def kernel(inp, out, raw, dpk, dg, goff, cbuf, ubuf, inv, loc_sem, g_send, g_recv, c_send, c_recv, u_send, u_recv):
+def kernel(inp, out, raw, dpk, dg, goff, cbuf, utop, ubuf, inv, loc_sem, g_send, g_recv, c_send, c_recv, u_send, u_recv):
     row = lax.axis_index("row")
     y = lax.axis_index("col")
     x = row // 2
@@ -33,8 +40,8 @@
     local = {g: [take(b, b, raw.at[b], loc_sem.at[b]) for b in DIAG[g]] for g in DIAG}
     for g in OFF:
         local[g] = [take(bi, bj, goff.at[OFF_AT[bi, bj], y, c, :, x], loc_sem.at[6 + OFF_AT[bi, bj]]) for bi, bj in OFF[g]]
-    local_c = [[take(3 + k, j, cbuf.at[j, k, c, :, x], loc_sem.at[12 + 3 * j + k]) for k in range(3)] for j in range(3)]
-    for grp in (local[DB], local[BO], local[DA], local_c[2], local_c[1], local_c[0], local[AO]):
+    local_c = [[take(bi, bj, cbuf.at[c_at(bi, bj), c, :, x], loc_sem.at[12 + c_at(bi, bj)]) for bi, bj in grp] for grp in CGRP]
+    for grp in (local[BO], local[DB], local[DA], local_c[3], local_c[1], local_c[2], local[AO], local_c[0]):
         for cp in grp:
             cp.start()
 
@@ -126,28 +133,31 @@
         gwait(g, 5, slot(g, x, co, yo))
         gwait(g, 6, slot(g, xo, co, yo))
 
-    def c_slot(j, sx, sc):
-        return cbuf.at[j, :, sc, :, sx]
-
-    def c_own(j):
-        for cp in local_c[j]:
+    def c_slot(g, sx, sc):
+        return cbuf.at[pl.ds(c_at(*CGRP[g][0]), len(CGRP[g])), sc, :, sx]
+
+    def c_own(g):
+        for cp in local_c[g]:
             cp.wait()
         for k, dev in enumerate((xnb, sib)):
-            start(copy(c_slot(j, x, c), c_send.at[j, k], c_recv.at[j, k], dev))
-
-    def c_relay(j):
-        copy(c_slot(j, xo, c), c_send.at[j, 0], c_recv.at[j, 0], sib).wait_recv()
-        start(copy(c_slot(j, xo, c), c_send.at[j, 2], c_recv.at[j, 2], sib))
-
-    def c_wait(j):
-        copy(c_slot(j, x, co), c_send.at[j, 1], c_recv.at[j, 1], sib).wait_recv()
-        copy(c_slot(j, xo, co), c_send.at[j, 2], c_recv.at[j, 2], sib).wait_recv()
-
-    def u_send_to(j):
-        start(copy(ubuf.at[j, y], u_send.at[j], u_recv.at[j], ynb))
-
-    def u_wait(j):
-        copy(ubuf.at[j, yo], u_send.at[j], u_recv.at[j], ynb).wait_recv()
+            start(copy(c_slot(g, x, c), c_send.at[g, k], c_recv.at[g, k], dev))
+
+    def c_relay(g):
+        copy(c_slot(g, xo, c), c_send.at[g, 0], c_recv.at[g, 0], sib).wait_recv()
+        start(copy(c_slot(g, xo, c), c_send.at[g, 2], c_recv.at[g, 2], sib))
+
+    def c_wait(g):
+        copy(c_slot(g, x, co), c_send.at[g, 1], c_recv.at[g, 1], sib).wait_recv()
+        copy(c_slot(g, xo, co), c_send.at[g, 2], c_recv.at[g, 2], sib).wait_recv()
+
+    def u_slot(g, sy):
+        return utop.at[sy] if g == 3 else ubuf.at[g, sy]
+
+    def u_send_to(g):
+        start(copy(u_slot(g, y), u_send.at[g], u_recv.at[g], ynb))
+
+    def u_wait(g):
+        copy(u_slot(g, yo), u_send.at[g], u_recv.at[g], ynb).wait_recv()
 
     def base(at):
         sub3 = lax.broadcasted_iota(jnp.int32, (3, 8, 128), 1)
@@ -307,54 +317,66 @@
         for w in (1, 2, 4):
             double(DIAG[g], w)
 
+    def c_block(k, j):
+        return cbuf[c_at(k, j)].reshape(256, 128)
+
+    def u_compute_top():
+        prod = hdot(z_diag(3), jnp.concatenate([c_block(3, j) for j in range(3)], axis=1))
+        for j in range(3):
+            utop[y, j] = prod[:, 128 * j:128 * j + 128]
+
     def u_compute(j):
-        acc = [None] * 6
-        for k in (3, 4, 5):
-            prod = hdot(zst[k], cbuf[j, k - 3].reshape(256, 128))
-            for i in range(k, 6):
-                part = prod[64 * (i - k):64 * (i - k) + 64]
-                acc[i] = part if acc[i] is None else acc[i] + part
-        for i in (3, 4, 5):
-            ubuf[j, y, 64 * (i - 3):64 * (i - 3) + 64] = acc[i]
+        both_rows = hdot(zst[3][64:192], c_block(3, j)) + hdot(zst[4], c_block(4, j))
+        ubuf[j, y, 0:64] = both_rows[0:64]
+        ubuf[j, y, 64:128] = both_rows[64:128] + hdot(zst[5], c_block(5, j))
 
     def u_add(j, acc):
-        for i in (3, 4, 5):
-            part = both(lambda q: ubuf[j, q, 64 * (i - 3):64 * (i - 3) + 64])
+        parts = {3: both(lambda q: utop[q, j]), 4: both(lambda q: ubuf[j, q, 0:64]), 5: both(lambda q: ubuf[j, q, 64:128])}
+        for i, part in parts.items():
             acc[i] = part if acc[i] is None else acc[i] + part
 
+    ready(BO)
+    pl.semaphore_wait(barrier, 3)
+    own(BO, "y")
     pack(DB)
-    pl.semaphore_wait(barrier, 3)
-    own(DB, "xys")
-    ready(BO)
-    own(BO, "xys")
+    own(DB, "xy")
+    own(BO, "x")
     pack(DA)
-    own(DA, "xs")
-    c_own(2)
     for i in range(5):
         out[64 * i:64 * i + 64, 128 * (i + 1):768] = jnp.zeros((64, 128 * (5 - i)), F32)
+    own(DB, "s")
     from_x(DB)
+    own(DA, "xs")
+    own(BO, "s")
+    c_own(3)
     own(DA, "y")
+    from_y(BO)
+    from_x(BO)
     from_y(DB)
+    from_diag(DB)
     c_own(1)
-    c_own(0)
-    from_x(BO)
-    from_y(BO)
     from_x(DA)
+    c_own(2)
     ready(AO)
-    own(AO, "xys")
-    from_diag(DB)
+    own(AO, "ys")
     wait_sib(DB)
     unpack(DB)
     base(3)
+    c_own(0)
+    double(DIAG[DB], 1)
+    c_relay(3)
+    double(DIAG[DB], 2)
+    from_diag(BO)
+    double(DIAG[DB], 4)
+    c_wait(3)
     from_y(DA)
+    own(AO, "x")
+    u_compute_top()
+    u_send_to(3)
+    from_diag(DA)
     c_relay(2)
-    double(DIAG[DB], 1)
-    from_diag(BO)
-    double(DIAG[DB], 2)
+    wait_sib(BO)
     c_relay(1)
-    double(DIAG[DB], 4)
-    from_diag(DA)
-    wait_sib(BO)
     finish(5, None)
     acc = [None] * 6
     add_terms(4, (5,), acc)
@@ -362,9 +384,10 @@
     acc = [None] * 6
     add_terms(3, (5, 4), acc)
     finish(3, acc)
-    c_relay(0)
     wait_sib(DA)
     c_wait(2)
+    c_relay(0)
+    from_y(AO)
     unpack(DA)
     u_compute(2)
     base(0)
@@ -373,15 +396,15 @@
     u_compute(1)
     double(DIAG[DA], 1)
     u_send_to(1)
-    from_y(AO)
     c_wait(0)
+    from_x(AO)
     u_compute(0)
     double(DIAG[DA], 2)
     u_send_to(0)
-    from_x(AO)
     double(DIAG[DA], 4)
     from_diag(AO)
     emit(0, 0, inv[0, y, c, :, x].reshape(64, 128))
+    u_wait(3)
     u_wait(2)
     acc = [None] * 6
     u_add(2, acc)
@@ -389,15 +412,15 @@
     wait_sib(AO)
     acc = [None] * 6
     add_terms(1, (2,), acc)
+    first = [None] * 6
+    add_terms(0, (2,), first)
     u_wait(1)
     u_add(1, acc)
     finish(1, acc)
-    acc = [None] * 6
-    add_terms(0, (2, 1), acc)
-    finish_first(acc, 1, 3)
+    add_terms(0, (1,), first)
     u_wait(0)
-    u_add(0, acc)
-    finish_first(acc, 3, 6)
+    u_add(0, first)
+    finish_first(first, 1, 6)
 
     for cp in sends:
         cp.wait_send()
@@ -418,16 +441,17 @@
                 pltpu.VMEM((2, 2, 2, 2, 15, 8, 128), F32),
                 pltpu.VMEM((6, 2, 2, 8, 2, 8, 128), F32),
                 pltpu.VMEM((6, 2, 2, 8, 2, 8, 128), F32),
-                pltpu.VMEM((3, 3, 2, 8, 2, 8, 128), F32),
-                pltpu.VMEM((3, 2, 192, 128), F32),
+                pltpu.VMEM((9, 2, 8, 2, 8, 128), F32),
+                pltpu.VMEM((2, 3, 64, 128), F32),
+                pltpu.VMEM((3, 2, 128, 128), F32),
                 pltpu.VMEM((6, 2, 2, 8, 2, 8, 128), F32),
                 pltpu.SemaphoreType.DMA((21,)),
                 pltpu.SemaphoreType.DMA((4, 7)),
                 pltpu.SemaphoreType.DMA((4, 7)),
-                pltpu.SemaphoreType.DMA((3, 3)),
-                pltpu.SemaphoreType.DMA((3, 3)),
-                pltpu.SemaphoreType.DMA((3,)),
-                pltpu.SemaphoreType.DMA((3,)),
+                pltpu.SemaphoreType.DMA((4, 3)),
+                pltpu.SemaphoreType.DMA((4, 3)),
+                pltpu.SemaphoreType.DMA((4,)),
+                pltpu.SemaphoreType.DMA((4,)),
             ],
             compiler_params=pltpu.CompilerParams(
                 collective_id=0, has_side_effects=True, vmem_limit_bytes=40 * 1024 * 1024),

time: 29.3 us -> 27.3 us (0.932)
  Pallas kernels: 28.1 us -> 26.1 us
    pallas_call x1, Pallas kernels: 28.1 us -> 26.1 us  [body(): pl.pallas_call(kernel, out_shape=jax.ShapeDtypeStruct((rows, cols), F32),...]
where the time goes in v7:
time: 27.3 us; the launch traced here: 27.1 us
  Pallas kernels  26.1 us (96%)
  local copies, waits for them, and re-layouts  1.02 us (4%)
    pallas_call x1, Pallas kernels, body(): pl.pallas_call(kernel, out_shape=jax.ShapeDtypeStruct((rows, cols), F32),...  26.1 us
    unnamed x1, local copies, waits for them, and re-layouts  1.02 us

profile of v7, /device:TPU:0, one launch (start us, length us, event | category | flops | bytes accessed | tf_op | source)
XLA Modules:
  0.0 27.1 jit_solution(12706881935322019169)
XLA Ops:
  0.0 26.1 %shard_map.17 = f32[384,768]{1,0:T(8,128)S(1)} custom-call(f32[48,8,768]{2,1,0:T(8,128)} %bitcast.1), custom_call_target="tpu_custom_call" | custom-call | tf_op jit(solution)/shard_map/pallas_call | solution.py:434
  26.1 1.0 %copy.3 = f32[384,768]{1,0:T(8,128)} copy(f32[384,768]{1,0:T(8,128)S(1)} %shard_map.17) | data formatting | bytes 2359296

commit v8 on v7

--- a/solution.py
+++ b/solution.py
@@ -7,10 +7,11 @@
 
 MESH = pl.DeviceIdType.MESH
 F32 = jnp.float32
-DB, DA, BO, AO = range(4)
+DB, DA, BO, A1, A2 = range(5)
 DIAG = {DB: (5, 4, 3), DA: (2, 1, 0)}
-OFF = {BO: ((5, 4), (4, 3), (5, 3)), AO: ((2, 1), (1, 0), (2, 0))}
-OFF_AT = {blk: 3 * (g - 2) + i for g, grp in OFF.items() for i, blk in enumerate(grp)}
+OFF = {BO: ((5, 4), (4, 3), (5, 3)), A1: ((2, 1),), A2: ((1, 0), (2, 0))}
+OFF_AT = {blk: n for n, blk in enumerate(blk for grp in OFF.values() for blk in grp)}
+VIA = {DB: "y", DA: "y", BO: "y", A1: "x", A2: "x"}
 
 
 CGRP = [[(4, j), (5, j)] for j in range(3)] + [[(3, j) for j in range(3)]]
@@ -41,7 +42,7 @@
     for g in OFF:
         local[g] = [take(bi, bj, goff.at[OFF_AT[bi, bj], y, c, :, x], loc_sem.at[6 + OFF_AT[bi, bj]]) for bi, bj in OFF[g]]
     local_c = [[take(bi, bj, cbuf.at[c_at(bi, bj), c, :, x], loc_sem.at[12 + c_at(bi, bj)]) for bi, bj in grp] for grp in CGRP]
-    for grp in (local[BO], local[DB], local[DA], local_c[3], local_c[1], local_c[2], local[AO], local_c[0]):
+    for grp in (local[DB], local[BO], local[DA], local_c[3], local_c[2], local[A1], local_c[1], local_c[0], local[A2]):
         for cp in grp:
             cp.start()
 
@@ -82,10 +83,12 @@
                         tiles = turn(tiles, 16 * (lb + 1)).reshape(2, 2, 8, 128)
                     dg[b, qc, :, lb] = tiles
 
-    def slot(g, sx, sc, sy):
+    def slot(g, sx, sc, sy, half=None):
         if g in DIAG:
-            return dpk.at[g, sy, sc, sx]
-        return goff.at[pl.ds(3 * (g - 2), 3), sy, sc, :, sx]
+            lo, num = (0, 15) if half is None else ((0, 8), (8, 7))[half]
+            return dpk.at[g, sy, sc, sx, pl.ds(lo, num)]
+        lo, num = (0, 8) if half is None else (4 * half, 4)
+        return goff.at[pl.ds(OFF_AT[OFF[g][0]], len(OFF[g])), sy, sc, pl.ds(lo, num), sx]
 
     sends = []
 
@@ -113,25 +116,32 @@
 
     def from_x(g):
         gwait(g, 0, slot(g, xo, c, y))
-        if g != AO:
-            gsend(g, 3, slot(g, xo, c, y), ynb)
+        if VIA[g] != "x":
+            gsend(g, 3, slot(g, xo, c, y, 0 if VIA[g] == "h" else None), ynb)
         gsend(g, 4, slot(g, xo, c, y), sib)
 
     def from_y(g):
         gwait(g, 1, slot(g, x, c, yo))
-        if g == AO:
+        if VIA[g] == "x":
             gsend(g, 3, slot(g, x, c, yo), xnb)
+        elif VIA[g] == "h":
+            gsend(g, 7, slot(g, x, c, yo, 1), xnb)
         gsend(g, 5, slot(g, x, c, yo), sib)
 
+    def diag_parts(g):
+        return ((3, 6, 0), (7, 8, 1)) if VIA[g] == "h" else ((3, 6, None),)
+
     def from_diag(g):
-        gwait(g, 3, slot(g, xo, c, yo))
-        gsend(g, 6, slot(g, xo, c, yo), sib)
+        for got, to, half in diag_parts(g):
+            gwait(g, got, slot(g, xo, c, yo, half))
+            gsend(g, to, slot(g, xo, c, yo, half), sib)
 
     def wait_sib(g):
         gwait(g, 2, slot(g, x, co, y))
         gwait(g, 4, slot(g, xo, co, y))
         gwait(g, 5, slot(g, x, co, yo))
-        gwait(g, 6, slot(g, xo, co, yo))
+        for got, to, half in diag_parts(g):
+            gwait(g, to, slot(g, xo, co, yo, half))
 
     def c_slot(g, sx, sc):
         return cbuf.at[pl.ds(c_at(*CGRP[g][0]), len(CGRP[g])), sc, :, sx]
@@ -268,6 +278,23 @@
                 return hdot(lefts[0], rights[0])
             return hdot(jnp.concatenate(lefts, axis=1), twin(*rights))
 
+        here = [(lanes((w, 2, 8, 128)) >> shift) == 2 * p for p in pairs]
+
+        def wide_rows(temp):
+            temp = [temp[:, 128 * qc:128 * qc + 128].reshape(shape) for qc in range(2)]
+            return rows_of([both(lambda qc: jnp.where(here[p], temp[qc][q], 0.0).reshape(n, 128))
+                            for p in pairs for q in range(2)])
+
+        if w < 4:
+            temps = [hdot(low_left(b), rows_of([both(lambda qc: inv[b, qc, q, rows(p, 0)].reshape(n, 128))
+                                                for p in pairs for q in range(2)])) for b in group]
+            for b, temp in zip(group, temps):
+                prod = -hdot(low_inv(b), wide_rows(temp))
+                for qc in range(2):
+                    val = prod[:, 128 * qc:128 * qc + 128].reshape(shape)
+                    for p in pairs:
+                        inv[b, qc, :, rows(p, 1)] = jnp.where(even[p], val, inv[b, qc, :, rows(p, 1)])
+            return
         two_blocks = (group[:2], group[2:])
         temps = [product([low_left(b) for b in bs], [up_inv(b) for b in bs]) for bs in two_blocks]
         for bs, temp in zip(two_blocks, temps):
@@ -311,12 +338,6 @@
         for i in range(lo, hi):
             emit(i, 0, res[64 * (i - lo):64 * (i - lo) + 64])
 
-    def inverses(g):
-        unpack(g)
-        base(min(DIAG[g]))
-        for w in (1, 2, 4):
-            double(DIAG[g], w)
-
     def c_block(k, j):
         return cbuf[c_at(k, j)].reshape(256, 128)
 
@@ -335,47 +356,52 @@
         for i, part in parts.items():
             acc[i] = part if acc[i] is None else acc[i] + part
 
+    pack(DB)
+    pl.semaphore_wait(barrier, 3)
+    own(DB, "xy")
     ready(BO)
-    pl.semaphore_wait(barrier, 3)
-    own(BO, "y")
-    pack(DB)
-    own(DB, "xy")
-    own(BO, "x")
+    own(BO, "sx")
     pack(DA)
+    own(DA, "x")
     for i in range(5):
         out[64 * i:64 * i + 64, 128 * (i + 1):768] = jnp.zeros((64, 128 * (5 - i)), F32)
+    own(DA, "s")
+    ready(A1)
+    own(A1, "s")
+    c_own(3)
+    own(BO, "y")
     own(DB, "s")
+    c_own(2)
     from_x(DB)
-    own(DA, "xs")
-    own(BO, "s")
-    c_own(3)
+    from_y(DB)
     own(DA, "y")
     from_y(BO)
+    ready(A2)
+    own(A2, "s")
     from_x(BO)
-    from_y(DB)
     from_diag(DB)
     c_own(1)
+    own(A1, "x")
+    c_own(0)
     from_x(DA)
-    c_own(2)
-    ready(AO)
-    own(AO, "ys")
     wait_sib(DB)
     unpack(DB)
     base(3)
-    c_own(0)
+    own(A2, "x")
+    own(A1, "y")
     double(DIAG[DB], 1)
+    own(A2, "y")
     c_relay(3)
     double(DIAG[DB], 2)
     from_diag(BO)
     double(DIAG[DB], 4)
     c_wait(3)
     from_y(DA)
-    own(AO, "x")
     u_compute_top()
     u_send_to(3)
+    wait_sib(BO)
     from_diag(DA)
     c_relay(2)
-    wait_sib(BO)
     c_relay(1)
     finish(5, None)
     acc = [None] * 6
@@ -386,41 +412,46 @@
     finish(3, acc)
     wait_sib(DA)
     c_wait(2)
-    c_relay(0)
-    from_y(AO)
     unpack(DA)
     u_compute(2)
     base(0)
     u_send_to(2)
+    from_y(A1)
     c_wait(1)
+    from_x(A1)
+    c_relay(0)
+    from_y(A2)
     u_compute(1)
     double(DIAG[DA], 1)
     u_send_to(1)
     c_wait(0)
-    from_x(AO)
     u_compute(0)
     double(DIAG[DA], 2)
+    from_x(A2)
+    from_diag(A1)
     u_send_to(0)
     double(DIAG[DA], 4)
-    from_diag(AO)
     emit(0, 0, inv[0, y, c, :, x].reshape(64, 128))
     u_wait(3)
     u_wait(2)
     acc = [None] * 6
     u_add(2, acc)
     finish(2, acc)
-    wait_sib(AO)
+    from_diag(A2)
+    wait_sib(A1)
     acc = [None] * 6
     add_terms(1, (2,), acc)
-    first = [None] * 6
-    add_terms(0, (2,), first)
     u_wait(1)
     u_add(1, acc)
     finish(1, acc)
-    add_terms(0, (1,), first)
+    wait_sib(A2)
+    acc = [None] * 6
+    add_terms(0, (2, 1), acc)
+    acc[3] = acc[3] + both(lambda q: utop[q, 0])
+    finish_first(acc, 1, 4)
     u_wait(0)
-    u_add(0, first)
-    finish_first(first, 1, 6)
+    u_add(0, acc)
+    finish_first(acc, 4, 6)
 
     for cp in sends:
         cp.wait_send()
@@ -446,8 +477,8 @@
                 pltpu.VMEM((3, 2, 128, 128), F32),
                 pltpu.VMEM((6, 2, 2, 8, 2, 8, 128), F32),
                 pltpu.SemaphoreType.DMA((21,)),
-                pltpu.SemaphoreType.DMA((4, 7)),
-                pltpu.SemaphoreType.DMA((4, 7)),
+                pltpu.SemaphoreType.DMA((5, 9)),
+                pltpu.SemaphoreType.DMA((5, 9)),
                 pltpu.SemaphoreType.DMA((4, 3)),
                 pltpu.SemaphoreType.DMA((4, 3)),
                 pltpu.SemaphoreType.DMA((4,)),

time: 27.3 us -> 28.1 us (1.029)
  Pallas kernels: 26.1 us -> 26.9 us
    pallas_call x1, Pallas kernels: 26.1 us -> 26.9 us  [body(): pl.pallas_call(kernel, out_shape=jax.ShapeDtypeStruct((rows, cols), F32),...]
where the time goes in v8:
time: 28.1 us; the launch traced here: 27.9 us
  Pallas kernels  26.9 us (96%)
  local copies, waits for them, and re-layouts  1.02 us (4%)
    pallas_call x1, Pallas kernels, body(): pl.pallas_call(kernel, out_shape=jax.ShapeDtypeStruct((rows, cols), F32),...  26.9 us
    unnamed x1, local copies, waits for them, and re-layouts  1.02 us

profile of v8, /device:TPU:0, one launch (start us, length us, event | category | flops | bytes accessed | tf_op | source)
XLA Modules:
  0.0 27.9 jit_solution(3263108541675632417)
XLA Ops:
  0.0 26.9 %shard_map.17 = f32[384,768]{1,0:T(8,128)S(1)} custom-call(f32[48,8,768]{2,1,0:T(8,128)} %bitcast.1), custom_call_target="tpu_custom_call" | custom-call | tf_op jit(solution)/shard_map/pallas_call | solution.py:465
  26.9 1.0 %copy.3 = f32[384,768]{1,0:T(8,128)} copy(f32[384,768]{1,0:T(8,128)S(1)} %shard_map.17) | data formatting | bytes 2359296

commit v9 on v7

--- a/solution.py
+++ b/solution.py
@@ -7,10 +7,11 @@
 
 MESH = pl.DeviceIdType.MESH
 F32 = jnp.float32
-DB, DA, BO, AO = range(4)
+DB, DA, BO, A1, A2 = range(5)
 DIAG = {DB: (5, 4, 3), DA: (2, 1, 0)}
-OFF = {BO: ((5, 4), (4, 3), (5, 3)), AO: ((2, 1), (1, 0), (2, 0))}
-OFF_AT = {blk: 3 * (g - 2) + i for g, grp in OFF.items() for i, blk in enumerate(grp)}
+OFF = {BO: ((5, 4), (4, 3), (5, 3)), A1: ((2, 1), (2, 0)), A2: ((1, 0),)}
+OFF_AT = {blk: n for n, blk in enumerate(blk for grp in OFF.values() for blk in grp)}
+LAST_X = (A1, A2,)
 
 
 CGRP = [[(4, j), (5, j)] for j in range(3)] + [[(3, j) for j in range(3)]]
@@ -41,7 +42,7 @@
     for g in OFF:
         local[g] = [take(bi, bj, goff.at[OFF_AT[bi, bj], y, c, :, x], loc_sem.at[6 + OFF_AT[bi, bj]]) for bi, bj in OFF[g]]
     local_c = [[take(bi, bj, cbuf.at[c_at(bi, bj), c, :, x], loc_sem.at[12 + c_at(bi, bj)]) for bi, bj in grp] for grp in CGRP]
-    for grp in (local[BO], local[DB], local[DA], local_c[3], local_c[1], local_c[2], local[AO], local_c[0]):
+    for grp in (local[DB], local[BO], local[DA], local_c[3], local_c[2], local[A1], local_c[1], local_c[0], local[A2]):
         for cp in grp:
             cp.start()
 
@@ -85,7 +86,7 @@
     def slot(g, sx, sc, sy):
         if g in DIAG:
             return dpk.at[g, sy, sc, sx]
-        return goff.at[pl.ds(3 * (g - 2), 3), sy, sc, :, sx]
+        return goff.at[pl.ds(OFF_AT[OFF[g][0]], len(OFF[g])), sy, sc, :, sx]
 
     sends = []
 
@@ -113,13 +114,13 @@
 
     def from_x(g):
         gwait(g, 0, slot(g, xo, c, y))
-        if g != AO:
+        if g not in LAST_X:
             gsend(g, 3, slot(g, xo, c, y), ynb)
         gsend(g, 4, slot(g, xo, c, y), sib)
 
     def from_y(g):
         gwait(g, 1, slot(g, x, c, yo))
-        if g == AO:
+        if g in LAST_X:
             gsend(g, 3, slot(g, x, c, yo), xnb)
         gsend(g, 5, slot(g, x, c, yo), sib)
 
@@ -128,10 +129,8 @@
         gsend(g, 6, slot(g, xo, c, yo), sib)
 
     def wait_sib(g):
-        gwait(g, 2, slot(g, x, co, y))
-        gwait(g, 4, slot(g, xo, co, y))
-        gwait(g, 5, slot(g, x, co, yo))
-        gwait(g, 6, slot(g, xo, co, yo))
+        for k, ref in ((2, slot(g, x, co, y)), (4, slot(g, xo, co, y)), (5, slot(g, x, co, yo)), (6, slot(g, xo, co, yo))):
+            gwait(g, k, ref)
 
     def c_slot(g, sx, sc):
         return cbuf.at[pl.ds(c_at(*CGRP[g][0]), len(CGRP[g])), sc, :, sx]
@@ -268,6 +267,23 @@
                 return hdot(lefts[0], rights[0])
             return hdot(jnp.concatenate(lefts, axis=1), twin(*rights))
 
+        here = [(lanes((w, 2, 8, 128)) >> shift) == 2 * p for p in pairs]
+
+        def wide_rows(temp):
+            temp = [temp[:, 128 * qc:128 * qc + 128].reshape(shape) for qc in range(2)]
+            return rows_of([both(lambda qc: jnp.where(here[p], temp[qc][q], 0.0).reshape(n, 128))
+                            for p in pairs for q in range(2)])
+
+        if w < 4:
+            temps = [hdot(low_left(b), rows_of([both(lambda qc: inv[b, qc, q, rows(p, 0)].reshape(n, 128))
+                                                for p in pairs for q in range(2)])) for b in group]
+            for b, temp in zip(group, temps):
+                prod = -hdot(low_inv(b), wide_rows(temp))
+                for qc in range(2):
+                    val = prod[:, 128 * qc:128 * qc + 128].reshape(shape)
+                    for p in pairs:
+                        inv[b, qc, :, rows(p, 1)] = jnp.where(even[p], val, inv[b, qc, :, rows(p, 1)])
+            return
         two_blocks = (group[:2], group[2:])
         temps = [product([low_left(b) for b in bs], [up_inv(b) for b in bs]) for bs in two_blocks]
         for bs, temp in zip(two_blocks, temps):
@@ -306,16 +322,13 @@
         for i in range(j + 1, 6):
             emit(i, j, mine[64 * (i - j - 1):64 * (i - j)])
 
-    def finish_first(acc, lo, hi):
-        res = -hdot(rows_of(acc[lo:hi]), inv[0, y].reshape(256, 128))
-        for i in range(lo, hi):
-            emit(i, 0, res[64 * (i - lo):64 * (i - lo) + 64])
-
-    def inverses(g):
-        unpack(g)
-        base(min(DIAG[g]))
-        for w in (1, 2, 4):
-            double(DIAG[g], w)
+    def empty():
+        return [None] * 6
+
+    def finish_first(acc):
+        res = -hdot(rows_of(acc[1:]), inv[0, y].reshape(256, 128))
+        for i in range(1, 6):
+            emit(i, 0, res[64 * (i - 1):64 * i])
 
     def c_block(k, j):
         return cbuf[c_at(k, j)].reshape(256, 128)
@@ -335,92 +348,99 @@
         for i, part in parts.items():
             acc[i] = part if acc[i] is None else acc[i] + part
 
+    pack(DB)
+    pl.semaphore_wait(barrier, 3)
+    own(DB, "yx")
     ready(BO)
-    pl.semaphore_wait(barrier, 3)
+    own(BO, "sx")
+    own(DB, "s")
     own(BO, "y")
-    pack(DB)
-    own(DB, "xy")
-    own(BO, "x")
+    from_x(DB)
     pack(DA)
+    own(DA, "yx")
+    from_y(DB)
+    c_own(3)
+    from_x(BO)
+    c_own(2)
+    own(DA, "s")
+    c_own(0)
     for i in range(5):
         out[64 * i:64 * i + 64, 128 * (i + 1):768] = jnp.zeros((64, 128 * (5 - i)), F32)
-    own(DB, "s")
-    from_x(DB)
-    own(DA, "xs")
-    own(BO, "s")
-    c_own(3)
-    own(DA, "y")
-    from_y(BO)
-    from_x(BO)
-    from_y(DB)
     from_diag(DB)
-    c_own(1)
+    wait_sib(DB)
+    from_y(DA)
     from_x(DA)
-    c_own(2)
-    ready(AO)
-    own(AO, "ys")
-    wait_sib(DB)
     unpack(DB)
     base(3)
-    c_own(0)
+    c_own(1)
     double(DIAG[DB], 1)
+    ready(A1)
+    own(A1, "y")
+    from_y(BO)
     c_relay(3)
     double(DIAG[DB], 2)
+    own(A1, "x")
     from_diag(BO)
+    ready(A2)
+    own(A2, "xy")
     double(DIAG[DB], 4)
     c_wait(3)
-    from_y(DA)
-    own(AO, "x")
     u_compute_top()
     u_send_to(3)
     from_diag(DA)
+    wait_sib(BO)
     c_relay(2)
-    wait_sib(BO)
-    c_relay(1)
     finish(5, None)
-    acc = [None] * 6
+    acc = empty()
     add_terms(4, (5,), acc)
     finish(4, acc)
-    acc = [None] * 6
+    acc = empty()
     add_terms(3, (5, 4), acc)
     finish(3, acc)
+    c_relay(1)
+    from_y(A1)
+    c_relay(0)
     wait_sib(DA)
     c_wait(2)
-    c_relay(0)
-    from_y(AO)
     unpack(DA)
     u_compute(2)
     base(0)
     u_send_to(2)
+    own(A1, "s")
+    own(A2, "s")
+    from_y(A2)
     c_wait(1)
     u_compute(1)
     double(DIAG[DA], 1)
     u_send_to(1)
     c_wait(0)
-    from_x(AO)
+    from_x(A2)
+    from_x(A1)
     u_compute(0)
     double(DIAG[DA], 2)
     u_send_to(0)
+    from_diag(A1)
     double(DIAG[DA], 4)
-    from_diag(AO)
     emit(0, 0, inv[0, y, c, :, x].reshape(64, 128))
+    from_diag(A2)
     u_wait(3)
     u_wait(2)
-    acc = [None] * 6
+    acc = empty()
     u_add(2, acc)
     finish(2, acc)
-    wait_sib(AO)
-    acc = [None] * 6
+    wait_sib(A1)
+    acc = empty()
     add_terms(1, (2,), acc)
-    first = [None] * 6
+    first = empty()
     add_terms(0, (2,), first)
     u_wait(1)
+    wait_sib(A2)
     u_add(1, acc)
     finish(1, acc)
     add_terms(0, (1,), first)
     u_wait(0)
     u_add(0, first)
-    finish_first(first, 1, 6)
+    finish_first(first)
 
     for cp in sends:
         cp.wait_send()
@@ -446,8 +466,8 @@
                 pltpu.VMEM((3, 2, 128, 128), F32),
                 pltpu.VMEM((6, 2, 2, 8, 2, 8, 128), F32),
                 pltpu.SemaphoreType.DMA((21,)),
-                pltpu.SemaphoreType.DMA((4, 7)),
-                pltpu.SemaphoreType.DMA((4, 7)),
+                pltpu.SemaphoreType.DMA((5, 7)),
+                pltpu.SemaphoreType.DMA((5, 7)),
                 pltpu.SemaphoreType.DMA((4, 3)),
                 pltpu.SemaphoreType.DMA((4, 3)),
                 pltpu.SemaphoreType.DMA((4,)),

time: 27.3 us -> 27.4 us (level)
  no operation moved by 1% of the time
where the time goes in v9:
time: 27.4 us; the launch traced here: 27.2 us
  Pallas kernels  26.2 us (96%)
  local copies, waits for them, and re-layouts  1.02 us (4%)
    pallas_call x1, Pallas kernels, body(): pl.pallas_call(kernel, out_shape=jax.ShapeDtypeStruct((rows, cols), F32),...  26.2 us
    unnamed x1, local copies, waits for them, and re-layouts  1.02 us

profile of v9, /device:TPU:0, one launch (start us, length us, event | category | flops | bytes accessed | tf_op | source)
XLA Modules:
  0.0 27.2 jit_solution(13004136246620306041)
XLA Ops:
  0.0 26.2 %shard_map.17 = f32[384,768]{1,0:T(8,128)S(1)} custom-call(f32[48,8,768]{2,1,0:T(8,128)} %bitcast.1), custom_call_target="tpu_custom_call" | custom-call | tf_op jit(solution)/shard_map/pallas_call | solution.py:454
  26.2 1.0 %copy.3 = f32[384,768]{1,0:T(8,128)} copy(f32[384,768]{1,0:T(8,128)S(1)} %shard_map.17) | data formatting | bytes 2359296

commit v10 on v9

--- a/solution.py
+++ b/solution.py
@@ -35,6 +35,10 @@
     xnb = {"row": 2 * xo + c}
     ynb = {"col": yo}
 
+    barrier = pltpu.get_barrier_semaphore()
+    for nbr in (sib, xnb, ynb):
+        pl.semaphore_signal(barrier, inc=1, device_id=nbr, device_id_type=MESH)
+
     def take(bi, bj, dst, sem):
         return pltpu.make_async_copy(inp.at[pl.ds(8 * bi, 8), :, pl.ds(128 * bj, 128)], dst, sem)
 
@@ -45,10 +49,6 @@
     for grp in (local[DB], local[BO], local[DA], local_c[3], local_c[2], local[A1], local_c[1], local_c[0], local[A2]):
         for cp in grp:
             cp.start()
-
-    barrier = pltpu.get_barrier_semaphore()
-    for nbr in (sib, xnb, ynb):
-        pl.semaphore_signal(barrier, inc=1, device_id=nbr, device_id_type=MESH)
 
     sub = lax.broadcasted_iota(jnp.int32, (8, 128), 0)
     lane = lax.broadcasted_iota(jnp.int32, (8, 128), 1)
@@ -352,44 +352,49 @@
     pl.semaphore_wait(barrier, 3)
     own(DB, "yx")
     ready(BO)
-    own(BO, "sx")
-    own(DB, "s")
-    own(BO, "y")
+    own(BO, "yx")
     from_x(DB)
     pack(DA)
-    own(DA, "yx")
+    own(DA, "x")
+    c_own(3)
+    own(BO, "s")
+    own(DA, "s")
+    ready(A2)
+    own(A2, "s")
+    c_own(2)
+    c_own(1)
     from_y(DB)
-    c_own(3)
+    own(DA, "y")
+    ready(A1)
+    own(A1, "s")
+    c_own(0)
+    own(A2, "x")
     from_x(BO)
-    c_own(2)
-    own(DA, "s")
-    c_own(0)
     for i in range(5):
         out[64 * i:64 * i + 64, 128 * (i + 1):768] = jnp.zeros((64, 128 * (5 - i)), F32)
+    own(DB, "s")
+    from_y(BO)
     from_diag(DB)
+    from_x(DA)
+    own(A1, "y")
+    from_y(DA)
+    own(A2, "y")
     wait_sib(DB)
-    from_y(DA)
-    from_x(DA)
     unpack(DB)
     base(3)
-    c_own(1)
     double(DIAG[DB], 1)
-    ready(A1)
-    own(A1, "y")
-    from_y(BO)
     c_relay(3)
     double(DIAG[DB], 2)
     own(A1, "x")
     from_diag(BO)
-    ready(A2)
-    own(A2, "xy")
     double(DIAG[DB], 4)
     c_wait(3)
     u_compute_top()
+    c_relay(2)
+    from_diag(DA)
     u_send_to(3)
-    from_diag(DA)
+    c_relay(1)
     wait_sib(BO)
-    c_relay(2)
     finish(5, None)
     acc = empty()
     add_terms(4, (5,), acc)
@@ -397,25 +402,22 @@
     acc = empty()
     add_terms(3, (5, 4), acc)
     finish(3, acc)
-    c_relay(1)
-    from_y(A1)
-    c_relay(0)
     wait_sib(DA)
     c_wait(2)
+    from_y(A1)
     unpack(DA)
     u_compute(2)
     base(0)
     u_send_to(2)
-    own(A1, "s")
-    own(A2, "s")
+    c_relay(0)
     from_y(A2)
+    from_x(A2)
     c_wait(1)
     u_compute(1)
     double(DIAG[DA], 1)
     u_send_to(1)
+    from_x(A1)
     c_wait(0)
-    from_x(A2)
-    from_x(A1)
     u_compute(0)
     double(DIAG[DA], 2)
     u_send_to(0)

time: 27.4 us -> 27.6 us (level)
  no operation moved by 1% of the time
where the time goes in v10:
time: 27.6 us; the launch traced here: 27.4 us
  Pallas kernels  26.4 us (96%)
  local copies, waits for them, and re-layouts  1.02 us (4%)
    pallas_call x1, Pallas kernels, body(): pl.pallas_call(kernel, out_shape=jax.ShapeDtypeStruct((rows, cols), F32),...  26.4 us
    unnamed x1, local copies, waits for them, and re-layouts  1.02 us

profile of v10, /device:TPU:0, one launch (start us, length us, event | category | flops | bytes accessed | tf_op | source)
XLA Modules:
  0.0 27.4 jit_solution(2805908324123385158)
XLA Ops:
  0.0 26.4 %shard_map.17 = f32[384,768]{1,0:T(8,128)S(1)} custom-call(f32[48,8,768]{2,1,0:T(8,128)} %bitcast.1), custom_call_target="tpu_custom_call" | custom-call | tf_op jit(solution)/shard_map/pallas_call | solution.py:456
  26.4 1.0 %copy.3 = f32[384,768]{1,0:T(8,128)} copy(f32[384,768]{1,0:T(8,128)S(1)} %shard_map.17) | data formatting | bytes 2359296

commit v11 on v7

--- a/solution.py
+++ b/solution.py
@@ -268,6 +268,23 @@
                 return hdot(lefts[0], rights[0])
             return hdot(jnp.concatenate(lefts, axis=1), twin(*rights))
 
+        here = [(lanes((w, 2, 8, 128)) >> shift) == 2 * p for p in pairs]
+
+        def wide_rows(temp):
+            temp = [temp[:, 128 * qc:128 * qc + 128].reshape(shape) for qc in range(2)]
+            return rows_of([both(lambda qc: jnp.where(here[p], temp[qc][q], 0.0).reshape(n, 128))
+                            for p in pairs for q in range(2)])
+
+        if w < 4:
+            temps = [hdot(low_left(b), rows_of([both(lambda qc: inv[b, qc, q, rows(p, 0)].reshape(n, 128))
+                                                for p in pairs for q in range(2)])) for b in group]
+            for b, temp in zip(group, temps):
+                prod = -hdot(low_inv(b), wide_rows(temp))
+                for qc in range(2):
+                    val = prod[:, 128 * qc:128 * qc + 128].reshape(shape)
+                    for p in pairs:
+                        inv[b, qc, :, rows(p, 1)] = jnp.where(even[p], val, inv[b, qc, :, rows(p, 1)])
+            return
         two_blocks = (group[:2], group[2:])
         temps = [product([low_left(b) for b in bs], [up_inv(b) for b in bs]) for bs in two_blocks]
         for bs, temp in zip(two_blocks, temps):
@@ -310,12 +327,6 @@
         res = -hdot(rows_of(acc[lo:hi]), inv[0, y].reshape(256, 128))
         for i in range(lo, hi):
             emit(i, 0, res[64 * (i - lo):64 * (i - lo) + 64])
-
-    def inverses(g):
-        unpack(g)
-        base(min(DIAG[g]))
-        for w in (1, 2, 4):
-            double(DIAG[g], w)
 
     def c_block(k, j):
         return cbuf[c_at(k, j)].reshape(256, 128)

time: 27.3 us -> 27.3 us (level)
  no operation moved by 1% of the time
where the time goes in v11:
time: 27.3 us; the launch traced here: 27.2 us
  Pallas kernels  26.1 us (96%)
  local copies, waits for them, and re-layouts  1.02 us (4%)
    pallas_call x1, Pallas kernels, body(): pl.pallas_call(kernel, out_shape=jax.ShapeDtypeStruct((rows, cols), F32),...  26.1 us
    unnamed x1, local copies, waits for them, and re-layouts  1.02 us

profile of v11, /device:TPU:0, one launch (start us, length us, event | category | flops | bytes accessed | tf_op | source)
XLA Modules:
  0.0 27.2 jit_solution(13480224691935626804)
XLA Ops:
  0.0 26.1 %shard_map.17 = f32[384,768]{1,0:T(8,128)S(1)} custom-call(f32[48,8,768]{2,1,0:T(8,128)} %bitcast.1), custom_call_target="tpu_custom_call" | custom-call | tf_op jit(solution)/shard_map/pallas_call | solution.py:445
  26.2 1.0 %copy.3 = f32[384,768]{1,0:T(8,128)} copy(f32[384,768]{1,0:T(8,128)S(1)} %shard_map.17) | data formatting | bytes 2359296

commit v12 on v9

--- a/solution.py
+++ b/solution.py
@@ -23,6 +23,11 @@
 
 def hdot(left, right):
     return jnp.dot(left, right, precision=lax.Precision.HIGHEST, preferred_element_type=F32)
+
+
+def hdot2(left, right):
+    half = left.shape[0] // 16 * 8
+    return jnp.concatenate([hdot(left[:half], right), hdot(left[half:], right)], axis=0)
 
 
 def kernel(inp, out, raw, dpk, dg, goff, cbuf, utop, ubuf, inv, loc_sem, g_send, g_recv, c_send, c_recv, u_send, u_recv):
@@ -306,7 +311,7 @@
 
     def add_terms(j, ks, acc):
         for k in ks:
-            prod = hdot(zst[k], low_block(k, j))
+            prod = (hdot2 if k == j + 1 else hdot)(zst[k], low_block(k, j))
             for i in range(k, 6):
                 part = prod[64 * (i - k):64 * (i - k) + 64]
                 acc[i] = part if acc[i] is None else acc[i] + part
@@ -316,7 +321,7 @@
         if j == 5:
             zst[5] = z_diag(5)
             return
-        res = -hdot(rows_of(acc[j + 1:]), inv_full(j))
+        res = -hdot2(rows_of(acc[j + 1:]), inv_full(j))
         zst[j] = rows_of([z_diag(j), res])
         mine = jnp.where(y == 0, res[:, 0:128], res[:, 128:256])
         for i in range(j + 1, 6):
@@ -326,7 +331,7 @@
         return [None] * 6
 
     def finish_first(acc):
-        res = -hdot(rows_of(acc[1:]), inv[0, y].reshape(256, 128))
+        res = -hdot2(rows_of(acc[1:]), inv[0, y].reshape(256, 128))
         for i in range(1, 6):
             emit(i, 0, res[64 * (i - 1):64 * i])
 

time: 27.4 us -> 27.4 us (level)
  no operation moved by 1% of the time
where the time goes in v12:
time: 27.4 us; the launch traced here: 27.2 us
  Pallas kernels  26.2 us (96%)
  local copies, waits for them, and re-layouts  1.02 us (4%)
    pallas_call x1, Pallas kernels, body(): pl.pallas_call(kernel, out_shape=jax.ShapeDtypeStruct((rows, cols), F32),...  26.2 us
    unnamed x1, local copies, waits for them, and re-layouts  1.02 us

profile of v12, /device:TPU:0, one launch (start us, length us, event | category | flops | bytes accessed | tf_op | source)
XLA Modules:
  0.0 27.2 jit_solution(1010555811653983958)
XLA Ops:
  0.0 26.2 %shard_map.17 = f32[384,768]{1,0:T(8,128)S(1)} custom-call(f32[48,8,768]{2,1,0:T(8,128)} %bitcast.1), custom_call_target="tpu_custom_call" | custom-call | tf_op jit(solution)/shard_map/pallas_call | solution.py:459
  26.2 1.0 %copy.3 = f32[384,768]{1,0:T(8,128)} copy(f32[384,768]{1,0:T(8,128)S(1)} %shard_map.17) | data formatting | bytes 2359296

commit v13 on v12

--- a/solution.py
+++ b/solution.py
@@ -330,10 +330,10 @@
     def empty():
         return [None] * 6
 
-    def finish_first(acc):
-        res = -hdot2(rows_of(acc[1:]), inv[0, y].reshape(256, 128))
-        for i in range(1, 6):
-            emit(i, 0, res[64 * (i - 1):64 * i])
+    def finish_first(acc, rows):
+        res = -hdot(rows_of([acc[i] for i in rows]), inv[0, y].reshape(256, 128))
+        for n, i in enumerate(rows):
+            emit(i, 0, res[64 * n:64 * n + 64])
 
     def c_block(k, j):
         return cbuf[c_at(k, j)].reshape(256, 128)
@@ -348,9 +348,14 @@
         ubuf[j, y, 0:64] = both_rows[0:64]
         ubuf[j, y, 64:128] = both_rows[64:128] + hdot(zst[5], c_block(5, j))
 
-    def u_add(j, acc):
-        parts = {3: both(lambda q: utop[q, j]), 4: both(lambda q: ubuf[j, q, 0:64]), 5: both(lambda q: ubuf[j, q, 64:128])}
-        for i, part in parts.items():
+    def u_rows(i, j, q):
+        if i == 3:
+            return utop[q, j]
+        return ubuf[j, q, 64 * (i - 4):64 * (i - 3)]
+
+    def u_add(j, acc, rows=(3, 4, 5)):
+        for i in rows:
+            part = both(lambda q: u_rows(i, j, q))
             acc[i] = part if acc[i] is None else acc[i] + part
 
     pack(DB)
@@ -443,9 +448,11 @@
     u_add(1, acc)
     finish(1, acc)
     add_terms(0, (1,), first)
+    u_add(0, first, (3,))
+    finish_first(first, (1, 2, 3))
     u_wait(0)
-    u_add(0, first)
-    finish_first(first)
+    u_add(0, first, (4, 5))
+    finish_first(first, (4, 5))
 
     for cp in sends:
         cp.wait_send()

time: 27.4 us -> 27.2 us (level)
  no operation moved by 1% of the time
where the time goes in v13:
time: 27.2 us; the launch traced here: 27 us
  Pallas kernels  26 us (96%)
  local copies, waits for them, and re-layouts  1.02 us (4%)
    pallas_call x1, Pallas kernels, body(): pl.pallas_call(kernel, out_shape=jax.ShapeDtypeStruct((rows, cols), F32),...  26 us
    unnamed x1, local copies, waits for them, and re-layouts  1.02 us

profile of v13, /device:TPU:0, one launch (start us, length us, event | category | flops | bytes accessed | tf_op | source)
XLA Modules:
  0.0 27.0 jit_solution(15667327499758197509)
XLA Ops:
  0.0 26.0 %shard_map.17 = f32[384,768]{1,0:T(8,128)S(1)} custom-call(f32[48,8,768]{2,1,0:T(8,128)} %bitcast.1), custom_call_target="tpu_custom_call" | custom-call | tf_op jit(solution)/shard_map/pallas_call | solution.py:466
  26.0 1.0 %copy.3 = f32[384,768]{1,0:T(8,128)} copy(f32[384,768]{1,0:T(8,128)S(1)} %shard_map.17) | data formatting | bytes 2359296

commit v14 on v13

--- a/solution.py
+++ b/solution.py
@@ -71,21 +71,25 @@
         for cp in local[g]:
             cp.wait()
         for i, b in enumerate(DIAG[g]):
-            dpk[g, y, c, x, 5 * i] = raw[b, 7]
+            dpk[g, y, c, x, 4 * i] = raw[b, 7]
             for p in range(3):
                 n = 112 - 16 * p
-                dpk[g, y, c, x, 5 * i + 1 + p] = jnp.where(lane < n, raw[b, 6 - p], turn(raw[b, p], n))
-            dpk[g, y, c, x, 5 * i + 4] = raw[b, 3]
+                dpk[g, y, c, x, 4 * i + 1 + p] = jnp.where(lane < n, raw[b, 6 - p], turn(raw[b, p], n))
+        one, two, three = DIAG[g]
+        dpk[g, y, c, x, 12] = jnp.where(lane < 64, raw[one, 3], turn(raw[two, 3], 64))
+        dpk[g, y, c, x, 13] = raw[three, 3]
 
     def unpack(g):
         for i, b in enumerate(DIAG[g]):
             for qc in range(2):
                 for lb in range(8):
-                    if lb >= 3:
-                        tiles = dpk[g, qc, :, :, 5 * i + 7 - lb]
-                    else:
-                        tiles = dpk[g, qc, :, :, 5 * i + 1 + lb].reshape(32, 128)
-                        tiles = turn(tiles, 16 * (lb + 1)).reshape(2, 2, 8, 128)
+                    at = 4 * i + (7 - lb if lb > 3 else 1 + lb)
+                    n = 16 * (lb + 1)
+                    if lb == 3:
+                        at, n = 12 + i // 2, 64 * (i % 2)
+                    tiles = dpk[g, qc, :, :, at]
+                    if lb < 4 and n:
+                        tiles = turn(tiles.reshape(32, 128), n).reshape(2, 2, 8, 128)
                     dg[b, qc, :, lb] = tiles
 
     def slot(g, sx, sc, sy):
@@ -470,7 +474,7 @@
             out_specs=pl.BlockSpec(memory_space=pltpu.VMEM),
             scratch_shapes=[
                 pltpu.VMEM((6, 8, 8, 128), F32),
-                pltpu.VMEM((2, 2, 2, 2, 15, 8, 128), F32),
+                pltpu.VMEM((2, 2, 2, 2, 14, 8, 128), F32),
                 pltpu.VMEM((6, 2, 2, 8, 2, 8, 128), F32),
                 pltpu.VMEM((6, 2, 2, 8, 2, 8, 128), F32),
                 pltpu.VMEM((9, 2, 8, 2, 8, 128), F32),

time: 27.2 us -> 27 us (level)
  no operation moved by 1% of the time
where the time goes in v14:
time: 27 us; the launch traced here: 26.9 us
  Pallas kernels  25.8 us (96%)
  local copies, waits for them, and re-layouts  1.02 us (4%)
    pallas_call x1, Pallas kernels, body(): pl.pallas_call(kernel, out_shape=jax.ShapeDtypeStruct((rows, cols), F32),...  25.8 us
    unnamed x1, local copies, waits for them, and re-layouts  1.02 us

profile of v14, /device:TPU:0, one launch (start us, length us, event | category | flops | bytes accessed | tf_op | source)
XLA Modules:
  0.0 26.9 jit_solution(1496148633012265540)
XLA Ops:
  0.0 25.8 %shard_map.17 = f32[384,768]{1,0:T(8,128)S(1)} custom-call(f32[48,8,768]{2,1,0:T(8,128)} %bitcast.1), custom_call_target="tpu_custom_call" | custom-call | tf_op jit(solution)/shard_map/pallas_call | solution.py:470
  25.8 1.0 %copy.3 = f32[384,768]{1,0:T(8,128)} copy(f32[384,768]{1,0:T(8,128)S(1)} %shard_map.17) | data formatting | bytes 2359296

commit v15 on v14

--- a/solution.py
+++ b/solution.py
@@ -40,6 +40,10 @@
     xnb = {"row": 2 * xo + c}
     ynb = {"col": yo}
 
+    barrier = pltpu.get_barrier_semaphore()
+    for nbr in (sib, xnb, ynb):
+        pl.semaphore_signal(barrier, inc=1, device_id=nbr, device_id_type=MESH)
+
     def take(bi, bj, dst, sem):
         return pltpu.make_async_copy(inp.at[pl.ds(8 * bi, 8), :, pl.ds(128 * bj, 128)], dst, sem)
 
@@ -50,10 +54,6 @@
     for grp in (local[DB], local[BO], local[DA], local_c[3], local_c[2], local[A1], local_c[1], local_c[0], local[A2]):
         for cp in grp:
             cp.start()
-
-    barrier = pltpu.get_barrier_semaphore()
-    for nbr in (sib, xnb, ynb):
-        pl.semaphore_signal(barrier, inc=1, device_id=nbr, device_id_type=MESH)
 
     sub = lax.broadcasted_iota(jnp.int32, (8, 128), 0)
     lane = lax.broadcasted_iota(jnp.int32, (8, 128), 1)

time: 27 us -> 27 us (level)
  no operation moved by 1% of the time
where the time goes in v15:
time: 27 us; the launch traced here: 26.8 us
  Pallas kernels  25.8 us (96%)
  local copies, waits for them, and re-layouts  1.02 us (4%)
    pallas_call x1, Pallas kernels, body(): pl.pallas_call(kernel, out_shape=jax.ShapeDtypeStruct((rows, cols), F32),...  25.8 us
    unnamed x1, local copies, waits for them, and re-layouts  1.02 us

profile of v15, /device:TPU:0, one launch (start us, length us, event | category | flops | bytes accessed | tf_op | source)
XLA Modules:
  0.0 26.8 jit_solution(7715396200521378690)
XLA Ops:
  0.0 25.8 %shard_map.17 = f32[384,768]{1,0:T(8,128)S(1)} custom-call(f32[48,8,768]{2,1,0:T(8,128)} %bitcast.1), custom_call_target="tpu_custom_call" | custom-call | tf_op jit(solution)/shard_map/pallas_call | solution.py:470
  25.8 1.0 %copy.3 = f32[384,768]{1,0:T(8,128)} copy(f32[384,768]{1,0:T(8,128)S(1)} %shard_map.17) | data formatting | bytes 2359296

commit v16 on v15

--- a/solution.py
+++ b/solution.py
@@ -315,7 +315,7 @@
 
     def add_terms(j, ks, acc):
         for k in ks:
-            prod = (hdot2 if k == j + 1 else hdot)(zst[k], low_block(k, j))
+            prod = (hdot2 if k == 1 else hdot)(zst[k], low_block(k, j))
             for i in range(k, 6):
                 part = prod[64 * (i - k):64 * (i - k) + 64]
                 acc[i] = part if acc[i] is None else acc[i] + part
@@ -325,7 +325,7 @@
         if j == 5:
             zst[5] = z_diag(5)
             return
-        res = -hdot2(rows_of(acc[j + 1:]), inv_full(j))
+        res = -(hdot2 if j < 3 else hdot)(rows_of(acc[j + 1:]), inv_full(j))
         zst[j] = rows_of([z_diag(j), res])
         mine = jnp.where(y == 0, res[:, 0:128], res[:, 128:256])
         for i in range(j + 1, 6):
@@ -432,9 +432,12 @@
     from_x(A1)
     u_compute(0)
     double(DIAG[DA], 2)
-    u_send_to(0)
+    last_u = copy(ubuf.at[0, y], u_send.at[0], u_recv.at[0], ynb)
+    sends.append(last_u)
+    pl.when(c == 0)(last_u.start)
     from_diag(A1)
     double(DIAG[DA], 4)
+    pl.when(c == 1)(last_u.start)
     emit(0, 0, inv[0, y, c, :, x].reshape(64, 128))
     from_diag(A2)
     u_wait(3)

time: 27 us -> 26.9 us (level)
  no operation moved by 1% of the time
where the time goes in v16:
time: 26.9 us; the launch traced here: 26.7 us
  Pallas kernels  25.7 us (96%)
  local copies, waits for them, and re-layouts  1.02 us (4%)
    pallas_call x1, Pallas kernels, body(): pl.pallas_call(kernel, out_shape=jax.ShapeDtypeStruct((rows, cols), F32),...  25.7 us
    unnamed x1, local copies, waits for them, and re-layouts  1.02 us

profile of v16, /device:TPU:0, one launch (start us, length us, event | category | flops | bytes accessed | tf_op | source)
XLA Modules:
  0.0 26.7 jit_solution(16165731208683237184)
XLA Ops:
  0.0 25.7 %shard_map.17 = f32[384,768]{1,0:T(8,128)S(1)} custom-call(f32[48,8,768]{2,1,0:T(8,128)} %bitcast.1), custom_call_target="tpu_custom_call" | custom-call | tf_op jit(solution)/shard_map/pallas_call | solution.py:473
  25.7 1.0 %copy.3 = f32[384,768]{1,0:T(8,128)} copy(f32[384,768]{1,0:T(8,128)S(1)} %shard_map.17) | data formatting | bytes 2359296

commit v17 on v16

--- a/solution.py
+++ b/solution.py
@@ -161,8 +161,11 @@
     def u_slot(g, sy):
         return utop.at[sy] if g == 3 else ubuf.at[g, sy]
 
+    def u_copy(g):
+        return copy(u_slot(g, y), u_send.at[g], u_recv.at[g], ynb)
+
     def u_send_to(g):
-        start(copy(u_slot(g, y), u_send.at[g], u_recv.at[g], ynb))
+        start(u_copy(g))
 
     def u_wait(g):
         copy(u_slot(g, yo), u_send.at[g], u_recv.at[g], ynb).wait_recv()
@@ -432,7 +435,7 @@
     from_x(A1)
     u_compute(0)
     double(DIAG[DA], 2)
-    last_u = copy(ubuf.at[0, y], u_send.at[0], u_recv.at[0], ynb)
+    last_u = u_copy(0)
     sends.append(last_u)
     pl.when(c == 0)(last_u.start)
     from_diag(A1)
@@ -470,6 +473,7 @@
 
     def body(local_l):
         rows, cols = local_l.shape
+        tiles = (2, 8, 2, 8, 128)
         return pl.pallas_call(
             kernel,
             out_shape=jax.ShapeDtypeStruct((rows, cols), F32),
@@ -478,12 +482,12 @@
             scratch_shapes=[
                 pltpu.VMEM((6, 8, 8, 128), F32),
                 pltpu.VMEM((2, 2, 2, 2, 14, 8, 128), F32),
-                pltpu.VMEM((6, 2, 2, 8, 2, 8, 128), F32),
-                pltpu.VMEM((6, 2, 2, 8, 2, 8, 128), F32),
-                pltpu.VMEM((9, 2, 8, 2, 8, 128), F32),
+                pltpu.VMEM((6, 2, *tiles), F32),
+                pltpu.VMEM((6, 2, *tiles), F32),
+                pltpu.VMEM((9, *tiles), F32),
                 pltpu.VMEM((2, 3, 64, 128), F32),
                 pltpu.VMEM((3, 2, 128, 128), F32),
-                pltpu.VMEM((6, 2, 2, 8, 2, 8, 128), F32),
+                pltpu.VMEM((6, 2, *tiles), F32),
                 pltpu.SemaphoreType.DMA((21,)),
                 pltpu.SemaphoreType.DMA((5, 7)),
                 pltpu.SemaphoreType.DMA((5, 7)),

time: 26.9 us -> 26.9 us (level)
  no operation moved by 1% of the time
where the time goes in v17:
time: 26.9 us; the launch traced here: 26.7 us
  Pallas kernels  25.7 us (96%)
  local copies, waits for them, and re-layouts  1.02 us (4%)
    pallas_call x1, Pallas kernels, body(): pl.pallas_call(kernel, out_shape=jax.ShapeDtypeStruct((rows, cols), F32),...  25.7 us
    unnamed x1, local copies, waits for them, and re-layouts  1.02 us

profile of v17, /device:TPU:0, one launch (start us, length us, event | category | flops | bytes accessed | tf_op | source)
XLA Modules:
  0.0 26.7 jit_solution(16165731208683237184)
XLA Ops:
  0.0 25.7 %shard_map.17 = f32[384,768]{1,0:T(8,128)S(1)} custom-call(f32[48,8,768]{2,1,0:T(8,128)} %bitcast.1), custom_call_target="tpu_custom_call" | custom-call | tf_op jit(solution)/shard_map/pallas_call | solution.py:477
  25.7 1.0 %copy.3 = f32[384,768]{1,0:T(8,128)} copy(f32[384,768]{1,0:T(8,128)S(1)} %shard_map.17) | data formatting | bytes 2359296

commit v18 on v17

--- a/solution.py
+++ b/solution.py
@@ -367,46 +367,49 @@
 
     pack(DB)
     pl.semaphore_wait(barrier, 3)
-    own(DB, "yx")
+    own(DB, "xy")
     ready(BO)
-    own(BO, "sx")
-    own(DB, "s")
-    own(BO, "y")
+    own(BO, "xy")
     from_x(DB)
     pack(DA)
-    own(DA, "yx")
+    own(DA, "x")
     from_y(DB)
+    own(DA, "s")
     c_own(3)
+    own(DB, "s")
+    c_own(2)
+    own(DA, "y")
     from_x(BO)
-    c_own(2)
-    own(DA, "s")
+    c_own(1)
+    from_diag(DB)
+    from_x(DA)
+    own(BO, "s")
+    ready(A1)
+    own(A1, "y")
     c_own(0)
     for i in range(5):
         out[64 * i:64 * i + 64, 128 * (i + 1):768] = jnp.zeros((64, 128 * (5 - i)), F32)
-    from_diag(DB)
+    from_y(BO)
+    from_y(DA)
+    ready(A2)
+    own(A2, "yx")
     wait_sib(DB)
-    from_y(DA)
-    from_x(DA)
     unpack(DB)
     base(3)
-    c_own(1)
     double(DIAG[DB], 1)
-    ready(A1)
-    own(A1, "y")
-    from_y(BO)
     c_relay(3)
     double(DIAG[DB], 2)
-    own(A1, "x")
     from_diag(BO)
-    ready(A2)
-    own(A2, "xy")
     double(DIAG[DB], 4)
+    own(A1, "s")
     c_wait(3)
     u_compute_top()
     u_send_to(3)
+    c_relay(2)
     from_diag(DA)
+    own(A1, "x")
+    c_relay(1)
     wait_sib(BO)
-    c_relay(2)
     finish(5, None)
     acc = empty()
     add_terms(4, (5,), acc)
@@ -414,30 +417,28 @@
     acc = empty()
     add_terms(3, (5, 4), acc)
     finish(3, acc)
-    c_relay(1)
     from_y(A1)
+    wait_sib(DA)
     c_relay(0)
-    wait_sib(DA)
     c_wait(2)
     unpack(DA)
     u_compute(2)
     base(0)
     u_send_to(2)
-    own(A1, "s")
+    from_x(A2)
+    c_wait(1)
     own(A2, "s")
     from_y(A2)
-    c_wait(1)
     u_compute(1)
     double(DIAG[DA], 1)
     u_send_to(1)
     c_wait(0)
-    from_x(A2)
-    from_x(A1)
     u_compute(0)
     double(DIAG[DA], 2)
     last_u = u_copy(0)
     sends.append(last_u)
     pl.when(c == 0)(last_u.start)
+    from_x(A1)
     from_diag(A1)
     double(DIAG[DA], 4)
     pl.when(c == 1)(last_u.start)

time: 26.9 us -> 27.1 us (level)
  no operation moved by 1% of the time
where the time goes in v18:
time: 27.1 us; the launch traced here: 26.9 us
  Pallas kernels  25.9 us (96%)
  local copies, waits for them, and re-layouts  1.02 us (4%)
    pallas_call x1, Pallas kernels, body(): pl.pallas_call(kernel, out_shape=jax.ShapeDtypeStruct((rows, cols), F32),...  25.9 us
    unnamed x1, local copies, waits for them, and re-layouts  1.02 us

profile of v18, /device:TPU:0, one launch (start us, length us, event | category | flops | bytes accessed | tf_op | source)
XLA Modules:
  0.0 26.9 jit_solution(3454209791787210057)
XLA Ops:
  0.0 25.9 %shard_map.17 = f32[384,768]{1,0:T(8,128)S(1)} custom-call(f32[48,8,768]{2,1,0:T(8,128)} %bitcast.1), custom_call_target="tpu_custom_call" | custom-call | tf_op jit(solution)/shard_map/pallas_call | solution.py:478
  25.9 1.0 %copy.3 = f32[384,768]{1,0:T(8,128)} copy(f32[384,768]{1,0:T(8,128)S(1)} %shard_map.17) | data formatting | bytes 2359296

commit v19 on v17

--- a/solution.py
+++ b/solution.py
@@ -338,7 +338,7 @@
         return [None] * 6
 
     def finish_first(acc, rows):
-        res = -hdot(rows_of([acc[i] for i in rows]), inv[0, y].reshape(256, 128))
+        res = -hdot2(rows_of([acc[i] for i in rows]), inv[0, y].reshape(256, 128))
         for n, i in enumerate(rows):
             emit(i, 0, res[64 * n:64 * n + 64])
 

time: 26.9 us -> 26.9 us (level)
  no operation moved by 1% of the time
where the time goes in v19:
time: 26.9 us; the launch traced here: 26.7 us
  Pallas kernels  25.7 us (96%)
  local copies, waits for them, and re-layouts  1.02 us (4%)
    pallas_call x1, Pallas kernels, body(): pl.pallas_call(kernel, out_shape=jax.ShapeDtypeStruct((rows, cols), F32),...  25.7 us
    unnamed x1, local copies, waits for them, and re-layouts  1.02 us

profile of v19, /device:TPU:0, one launch (start us, length us, event | category | flops | bytes accessed | tf_op | source)
XLA Modules:
  0.0 26.7 jit_solution(16842327988850987097)
XLA Ops:
  0.0 25.7 %shard_map.17 = f32[384,768]{1,0:T(8,128)S(1)} custom-call(f32[48,8,768]{2,1,0:T(8,128)} %bitcast.1), custom_call_target="tpu_custom_call" | custom-call | tf_op jit(solution)/shard_map/pallas_call | solution.py:477
  25.7 1.0 %copy.3 = f32[384,768]{1,0:T(8,128)} copy(f32[384,768]{1,0:T(8,128)S(1)} %shard_map.17) | data formatting | bytes 2359296
